TPU v7x, 512 devices: a whole 4x8x8 slice. The times are simulated.
512 devices in a mesh: gx: 8 (over x, core), gy: 8 (over y), gz: 8 (over z).
Axes of the slice: x: 4, y: 8, z: 8, core: 2. Of those that a mesh axis runs over, the one named last changes fastest.
Arguments:
- warped_image: float32 [512, 512, 1024], P('gx', 'gy', 'gz'), may hold values from -6 to 6
- fixed_image: float32 [512, 512, 1024], P('gx', 'gy', 'gz'), may hold values from -6 to 6
- fine_control: float32 [3, 64, 64, 128], P(None, 'gx', 'gy', 'gz'), may hold values from -6 to 6
- coarse_control: float32 [3, 16, 16, 32], replicated, may hold values from -6 to 6
Outputs:
- fine_gradient: float32 [3, 64, 64, 128], P(None, 'gx', 'gy', 'gz')
- coarse_gradient: float32 [3, 16, 16, 32], replicated
All inputs are finite; a program needn't handle non-finite values.
Results may differ from a plain program's by a relative error of at most 0.0003.
Values sent between devices are 32-bit elements; how exact they have to be, the bound alone decides.
A program may use at most 64 MiB of HBM per device.

v0:
```python
import itertools

import jax
import jax.numpy as jnp
import numpy as np
from jax import lax
from jax.experimental import pallas as pl
from jax.experimental.pallas import tpu as pltpu
from jax.sharding import PartitionSpec as P

SPF = 8
SPC = 32
BEND = 0.01
FB = 96
MESH = pl.DeviceIdType.MESH
F32 = jnp.float32
BF16 = jnp.bfloat16


def beta(t):
    m = np.abs(t)
    r = 2.0 - m
    return np.where(m < 1.0, 2.0 / 3.0 - m * m + 0.5 * m**3, np.where(m < 2.0, r**3 / 6.0, 0.0))


def basis(voxels, points, spacing, first):
    v = np.arange(voxels)[:, None] + 0.5
    c = (np.arange(points)[None, :] + first) * spacing + 0.5 * spacing
    return beta((v - c) / spacing)


def halves(w):
    hi = np.asarray(w, np.float32).astype(jnp.bfloat16)
    lo = (np.asarray(w, np.float64) - hi.astype(np.float64)).astype(np.float32).astype(jnp.bfloat16)
    return hi, lo


W4 = beta((np.arange(4)[:, None] + 4.5 - 4.0 * np.arange(4)[None, :]) / 4.0) / 24.0
TWO = np.array([1.0, 4.0, 6.0, 4.0, 1.0]) / 8.0


def spread(c, step):
    out = np.zeros((len(c) - 1) * step + 1)
    out[::step] = c
    return out


C29 = np.convolve(np.convolve(TWO, spread(TWO, 2)), spread(TWO, 4))


def y_matrix(sy):
    rows = np.zeros((24, sy))
    rows[:12] = basis(sy, 12, SPF, -2).T * SPF**-1.5
    rows[16:22] = basis(sy, 6, SPC, -2).T * SPC**-1.5
    hi, lo = halves(rows)
    return np.concatenate([np.concatenate([hi, hi], 1), np.concatenate([lo, lo], 1)], 0)


def z_matrices(sz):
    out = []
    for a in range(3):
        cols = np.zeros((sz, 128))
        cols[:, FB : FB + 20] = basis(sz, 20, SPF, -2)
        cols[:, 32 * a : 32 * a + 8] = basis(sz, 8, SPC, -2)
        hi, lo = halves(cols)
        half = np.concatenate([hi, lo], 1)
        out.append(np.concatenate([half, half], 0))
    return np.stack(out)


def d_matrix(sz):
    d = np.zeros((sz, sz), np.float32)
    for shift, value in ((-2, 1.0), (-1, -8.0), (1, 8.0), (2, -1.0)):
        for v in range(sz):
            if 0 <= v + shift < sz:
                d[v + shift, v] = value
    return np.concatenate([d, d], 0).astype(jnp.bfloat16)


def split(x):
    hi = x.astype(BF16)
    return hi, (x - hi.astype(F32)).astype(BF16)


def lanes(shape):
    return lax.broadcasted_iota(jnp.int32, shape, len(shape) - 1)


def roll(x, shift, axis):
    return pltpu.roll(x, shift % x.shape[axis] if isinstance(shift, int) else shift, axis)


def kernel(dims, w_hbm, f_hbm, ctl, cctl, wy, wz, dz_w, fine_out, coarse_out,
           wb, fb, sp, hys, hyr, hzs, hzr, cz, dzb, xs, zs, e, csend, crecv, zg, yg, xg,
           fxr, fys, fyr, fzs, fzr, fw,
           img_sem, hs, hr, cs, cr, gs, gr, fs, fr):
    nx, ny, nz = dims
    pos = (lax.axis_index("gx"), lax.axis_index("gy"), lax.axis_index("gz"))
    gx, gy, gz = pos
    has = [{-1: pos[i] > 0, 1: pos[i] < dims[i] - 1} for i in range(3)]

    def exists(d):
        cond = None
        for i in range(3):
            if d[i]:
                cond = has[i][d[i]] if cond is None else jnp.logical_and(cond, has[i][d[i]])
        return cond

    def at(d):
        return tuple(pos[i] + d[i] for i in range(3))

    def ring(axis, o):
        t = lax.rem(pos[axis] + o, dims[axis])
        return tuple(t if i == axis else pos[i] for i in range(3)), t

    neighbours = [d for d in itertools.product((-1, 0, 1), repeat=3) if any(d)]
    diagonal = [d for d in neighbours if sum(map(abs, d)) > 1]

    chunks = 8
    planes = 8
    for c in range(chunks):
        part = pl.ds(c * planes, planes)
        pltpu.make_async_copy(w_hbm.at[part], wb.at[part], img_sem.at[0, c]).start()
        pltpu.make_async_copy(f_hbm.at[part], fb.at[part], img_sem.at[1, c]).start()

    bar = pltpu.get_barrier_semaphore()
    for axis in range(3):
        for o in range(1, dims[axis]):
            pl.semaphore_signal(bar, inc=1, device_id=ring(axis, o)[0], device_id_type=MESH)
    for d in diagonal:
        @pl.when(exists(d))
        def _(d=d):
            pl.semaphore_signal(bar, inc=1, device_id=at(d), device_id_type=MESH)
    wide = [1 + h[-1].astype(jnp.int32) + h[1].astype(jnp.int32) for h in has]
    greeted = wide[0] * wide[1] * wide[2] - 1 - (wide[0] + wide[1] + wide[2] - 3) + (nx + ny + nz - 3)

    zero8 = jnp.zeros((8, 128), F32)
    for side, d in ((0, -1), (1, 1)):
        @pl.when(jnp.logical_not(has[0][d]))
        def _(side=side):
            sp[66 * side : 66 * side + 2, 8:72, :] = jnp.zeros((2, 64, 128), F32)
            fxr[side] = jnp.zeros(fxr.shape[1:], F32)

        @pl.when(jnp.logical_not(has[1][d]))
        def _(side=side):
            hyr[side] = jnp.zeros(hyr.shape[1:], F32)
            fyr[side] = jnp.zeros(fyr.shape[1:], F32)

        @pl.when(jnp.logical_not(has[2][d]))
        def _(side=side):
            hzr[side] = jnp.zeros(hzr.shape[1:], F32)
            fzr[side] = jnp.zeros(fzr.shape[1:], F32)

    hzs[...] = jnp.zeros(hzs.shape, F32)

    lane64 = lanes((64, 128))

    def sum_chunk(c, _):
        base = pl.multiple_of(c * planes, planes)
        part = pl.ds(base, planes)
        pltpu.make_async_copy(w_hbm.at[part], wb.at[part], img_sem.at[0, c]).wait()
        pltpu.make_async_copy(f_hbm.at[part], fb.at[part], img_sem.at[1, c]).wait()
        packed = jnp.zeros((64, 128), F32)
        for j in range(planes):
            w = wb[base + j]
            f = fb[base + j]
            s = w + f
            wb[base + j] = w - f
            sp[base + j + 2, 8:72, :] = s
            hys[0, base + j] = s[0:2]
            hys[1, base + j] = s[62:64]
            packed = jnp.where(lane64 // 4 == j, roll(s, 4 * j + 2, 1), packed)
            hi, lo = split(s)
            dzb[base + j] = jnp.dot(jnp.concatenate([hi, lo], 1), dz_w[...], preferred_element_type=F32)
        h = c // 4
        q = lax.rem(c, 4)
        hzs[h] = jnp.where(lane64 // 32 == q, pltpu.roll(packed, 32 * q, 1), hzs[h])
        return 0

    lax.fori_loop(0, chunks, sum_chunk, 0)
    pl.semaphore_wait(bar, greeted)

    def halo(k):
        axis, side = k // 2, k % 2
        d = [0, 0, 0]
        d[axis] = 2 * side - 1
        if axis == 0:
            src = sp.at[pl.ds(2 if side == 0 else 64, 2), pl.ds(8, 64), :]
            dst = sp.at[pl.ds(66 if side == 0 else 0, 2), pl.ds(8, 64), :]
        elif axis == 1:
            src, dst = hys.at[side], hyr.at[1 - side]
        else:
            src, dst = hzs, hzr.at[1 - side]
        return d, pltpu.make_async_remote_copy(
            src_ref=src, dst_ref=dst, send_sem=hs.at[k], recv_sem=hr.at[k],
            device_id=at(d), device_id_type=MESH)

    def fine_copy(k):
        axis, side = k // 2, k % 2
        d = [0, 0, 0]
        d[axis] = 2 * side - 1
        if axis == 0:
            src, dst = e.at[:, pl.ds(10 * side, 2)], fxr.at[1 - side]
        elif axis == 1:
            src, dst = fys.at[side], fyr.at[1 - side]
        else:
            src, dst = fzs.at[side], fzr.at[1 - side]
        return d, pltpu.make_async_remote_copy(
            src_ref=src, dst_ref=dst, send_sem=fs.at[k], recv_sem=fr.at[k],
            device_id=at(d), device_id_type=MESH)

    def start(make, k):
        d, copy = make(k)
        pl.when(exists(d))(lambda: copy.start())

    def sent(make, k):
        d, copy = make(k)
        pl.when(exists(d))(lambda: copy.wait_send())

    def arrived(make, k):
        d, copy = make(k)
        pl.when(exists([-v for v in d]))(lambda: copy.wait_recv())

    for k in (4, 5, 2, 3, 0, 1):
        start(halo, k)

    row16 = lax.broadcasted_iota(jnp.int32, (16, 128), 0)
    lane16 = lanes((16, 128))
    row_g = row16 - 2 + gy * 8
    lane_g = lane16 - (FB + 2) + gz * 16
    in_grid = (row_g >= 0) & (row_g < ny * 8) & (lane_g >= 0) & (lane_g < nz * 16)

    def lap(centre, low, high):
        total = roll(centre, 1, 0) + roll(centre, -1, 0) + roll(centre, 1, 1) + roll(centre, -1, 1)
        if low is not None:
            total = total + low
        if high is not None:
            total = total + high
        return total - 6.0 * centre

    def fine_bend(a, _):
        for j in range(8):
            block = jnp.concatenate([ctl[a, j], jnp.zeros((8, 112), F32)], 1)
            block = jnp.concatenate([block, zero8], 0)
            fw[j + 2] = roll(roll(block, 2, 0), FB + 2, 1)
        zero16 = jnp.zeros((16, 128), F32)
        for j in (0, 1, 10, 11):
            fw[j] = zero16
        first = []
        for j in range(12):
            if j in (0, 11):
                first.append(None)
                continue
            low = fw[j - 1] if 0 < j else None
            high = fw[j + 1] if j < 11 else None
            value = lap(fw[j], low, high)
            p = gx * 8 + j - 2
            ok = in_grid & (p >= 0) & (p < nx * 8)
            first.append(jnp.where(ok, value, 0.0))
        for j in range(12):
            centre = first[j] if first[j] is not None else zero16
            low = first[j - 1] if j > 0 else None
            high = first[j + 1] if j < 11 else None
            e[a, j] = BEND * lap(centre, low, high)
        return 0

    lax.fori_loop(0, 3, fine_bend, 0)

    kx, ky, kz = cctl.shape[1:]
    shape = (ky, kz)
    crow = lax.broadcasted_iota(jnp.int32, (ky, 128), 0)
    clane = lanes((ky, 128))

    def clap(centre, low, high):
        total = jnp.where(crow > 0, roll(centre, 1, 0), 0.0) + jnp.where(crow < ky - 1, roll(centre, -1, 0), 0.0)
        total = total + roll(centre, 1, 1) + roll(centre, -1, 1)
        if low is not None:
            total = total + low
        if high is not None:
            total = total + high
        return jnp.where(clane < kz, total - 6.0 * centre, 0.0)

    def coarse_bend(a, _):
        field = [jnp.concatenate([cctl[a, j], jnp.zeros((ky, 128 - kz), F32)], 1) for j in range(kx)]
        for _level in range(2):
            field = [clap(field[j], field[j - 1] if j else None, field[j + 1] if j < kx - 1 else None)
                     for j in range(kx)]
        for j in range(kx):
            coarse_out[a, j] = BEND * field[j][:, :kz]
        return 0

    lax.fori_loop(0, 3, coarse_bend, 0)

    for k in range(6):
        arrived(halo, k)

    def place_y(x, _):
        sp[x + 2, 6:8, :] = hyr[0, x]
        sp[x + 2, 72:74, :] = hyr[1, x]
        return 0

    lax.fori_loop(0, 64, place_y, 0, unroll=8)

    m4 = lane64 % 4
    for h in range(2):
        u = jnp.where(m4 < 2, hzr[0, h], hzr[1, h])
        a_part = jnp.where(m4 < 2, -roll(u, -2, 1), roll(u, 2, 1))
        b_part = jnp.where(m4 == 1, 8.0 * roll(u, -1, 1), jnp.where(m4 == 2, -8.0 * roll(u, 1, 1), 0.0))
        cz[h] = a_part + b_part
    edge = (lane64 < 2) | (lane64 >= 126)

    def z_fix(c, _):
        base = pl.multiple_of(c * planes, planes)
        q = lax.rem(c, 4)
        part = pltpu.roll(cz[c // 4], lax.rem(128 - 32 * q, 128), 1)
        for j in range(planes):
            dzb[base + j] = dzb[base + j] + jnp.where(edge, roll(part, -(4 * j + 2), 1), 0.0)
        return 0

    lax.fori_loop(0, chunks, z_fix, 0)

    groups = 16
    slabs = groups + 3

    def column(yt, _):
        r0 = pl.multiple_of(8 * yt, 8)

        def put(a, g, value):
            xs[pl.ds(r0, 8), pl.ds(pl.multiple_of((a * slabs + g) * 128, 128), 128)] = value

        def pair(gg, acc):
            acc = [list(row) for row in acc]
            x0 = 8 * gg
            c = [sp[x0 + i, pl.ds(r0 + 8, 8), :] for i in range(12)]
            for sub in range(2):
                for k in range(4):
                    i = 4 * sub + k
                    plane = x0 + i + 2
                    sx = (c[i] - c[i + 4]) + 8.0 * (c[i + 3] - c[i + 1])
                    ym2 = sp[plane, pl.ds(r0 + 6, 8), :]
                    ym1 = sp[plane, pl.ds(r0 + 7, 8), :]
                    yp1 = sp[plane, pl.ds(r0 + 9, 8), :]
                    yp2 = sp[plane, pl.ds(r0 + 10, 8), :]
                    sy = (ym2 - yp2) + 8.0 * (yp1 - ym1)
                    sz = dzb[x0 + i, pl.ds(r0, 8), :]
                    diff = wb[x0 + i, pl.ds(r0, 8), :]
                    for a, s in enumerate((sx, sy, sz)):
                        f = diff * s
                        for m in range(4):
                            acc[a][m] = acc[a][m] + float(W4[k, m]) * f
                for a in range(3):
                    put(a, 2 * gg + sub, acc[a][0])
                    acc[a] = [acc[a][1], acc[a][2], acc[a][3], jnp.zeros((8, 128), F32)]
            return tuple(tuple(row) for row in acc)

        acc = lax.fori_loop(0, groups // 2, pair, tuple(tuple(zero8 for _ in range(4)) for _ in range(3)))
        for a in range(3):
            for m in range(3):
                put(a, groups + m, acc[a][m])
        return 0

    lax.fori_loop(0, 8, column, 0)

    for a in range(3):
        x = xs[:, a * slabs * 128 : (a + 1) * slabs * 128]
        hi, lo = split(x)
        y = jnp.dot(wy[...], jnp.concatenate([hi, lo], 0), preferred_element_type=F32)
        y = y[:24] + y[24:]
        y = jnp.concatenate([y[:, 128 * i : 128 * (i + 1)] for i in range(slabs)], 0)
        hi, lo = split(y)
        z = jnp.dot(jnp.concatenate([hi, lo], 1), wz[a], preferred_element_type=F32)
        z = z[:, :128] + z[:, 128:]
        for i in range(slabs):
            zs[a, i] = z[24 * i : 24 * (i + 1)]

    total = [zs[0, i, 16:24, :] + zs[1, i, 16:24, :] + zs[2, i, 16:24, :] for i in range(slabs)]
    for jj in range(6):
        v = None
        for i in range(slabs):
            tap = i - 8 * jj + 25
            if 0 <= tap < 29:
                term = float(C29[tap]) * total[i]
                v = term if v is None else v + term
        for dy in range(3):
            csend[jj // 2, dy, jj % 2] = v[2 * dy : 2 * dy + 2]

    def coarse_copy(d):
        slot = 9 * (d[0] + 1) + 3 * (d[1] + 1) + d[2] + 1
        return pltpu.make_async_remote_copy(
            src_ref=csend.at[d[0] + 1, d[1] + 1], dst_ref=crecv.at[slot],
            send_sem=cs.at[slot], recv_sem=cr.at[slot], device_id=at(d), device_id_type=MESH)

    far_first = sorted(neighbours, key=lambda d: -sum(map(abs, d)))
    for d in far_first:
        pl.when(exists(d))(lambda d=d: coarse_copy(d).start())

    for a in range(3):
        for j in range(12):
            v = e[a, j]
            for k in range(5):
                i = 2 * j - 4 + k
                if 0 <= i < slabs:
                    v = v + float(TWO[k]) * zs[a, i, 0:16, :]
            e[a, j] = v
    for k in (0, 1):
        start(fine_copy, k)

    own = csend[1, 1]
    low = jnp.zeros((2, 2, 128), F32)
    high = jnp.zeros((2, 2, 128), F32)
    for d in sorted(neighbours, key=lambda d: sum(map(abs, d))):
        back = tuple(-v for v in d)
        pl.when(exists(back))(lambda d=d: coarse_copy(d).wait_recv())
        slot = 9 * (d[0] + 1) + 3 * (d[1] + 1) + d[2] + 1
        piece = jnp.where(exists(back), crecv[slot], 0.0)
        if d[2] == 0:
            own = own + piece
        elif d[2] == 1:
            low = low + piece
        else:
            high = high + piece
    l4 = lanes((2, 2, 128))
    r_in = l4 % 32
    inner = l4 < 96
    own = jnp.where(inner & (r_in >= 2) & (r_in < 6), own, 0.0)
    own = own + jnp.where(inner & (r_in >= 2) & (r_in < 4), roll(low, -4, 2), 0.0)
    own = own + jnp.where(inner & (r_in >= 4) & (r_in < 6), roll(high, 4, 2), 0.0)
    shift = lax.rem(4 * gz + 126, 128)
    zg[gz] = jnp.stack([pltpu.roll(own[i], shift, 1) for i in range(2)])

    def gather_copy(axis, o):
        device, _ = ring(axis, o)
        if axis == 2:
            src = dst = zg.at[gz]
        elif axis == 1:
            src = dst = yg.at[:, gy]
        else:
            src, dst = yg, xg.at[gx]
        return pltpu.make_async_remote_copy(
            src_ref=src, dst_ref=dst, send_sem=gs.at[axis, o], recv_sem=gr.at[axis, o],
            device_id=device, device_id_type=MESH)

    def offsets(axis):
        n = dims[axis]
        return sorted(range(1, n), key=lambda o: -min(o, n - o))

    def gather_start(axis):
        for o in offsets(axis):
            gather_copy(axis, o).start()

    def gather_wait(axis):
        n = dims[axis]
        for o in reversed(offsets(axis)):
            s = lax.rem(pos[axis] + n - o, n)
            dst = (xg.at[s], yg.at[:, s], zg.at[s])[axis]
            src = yg if axis == 0 else dst
            pltpu.make_async_remote_copy(
                src_ref=src, dst_ref=dst, send_sem=gs.at[axis, o], recv_sem=gr.at[axis, o],
                device_id=ring(axis, o)[0], device_id_type=MESH).wait_recv()

    gather_start(2)

    for k in (0, 1):
        sent(fine_copy, k)
        arrived(fine_copy, k)
    for a in range(3):
        for j in range(8):
            v = e[a, j + 2]
            if j < 2:
                v = v + fxr[0, a, j]
            if j >= 6:
                v = v + fxr[1, a, j - 6]
            e[a, j + 2] = v
            fys[0, 8 * a + j] = v[0:2]
            fys[1, 8 * a + j] = v[10:12]
    for k in (2, 3):
        start(fine_copy, k)

    gather_wait(2)
    line = zg[0]
    for s in range(1, nz):
        line = line + zg[s]
    yg[:, gy] = line
    gather_start(1)

    for k in (2, 3):
        arrived(fine_copy, k)
    lane8 = lanes((8, 128))
    pack0 = zero8
    pack1 = zero8
    zero4 = jnp.zeros((4, 128), F32)
    for a in range(3):
        for j in range(8):
            s = 8 * a + j
            v = e[a, j + 2]
            edges = jnp.concatenate([fyr[0, s], zero4, fyr[1, s]], 0)
            v = roll(v, -2, 0)[0:8] + edges
            e[a, j + 2, 0:8, :] = v
            turned = roll(v, 2 * s - FB, 1)
            pack0 = jnp.where(lane8 // 2 == s, turned, pack0)
            pack1 = jnp.where(lane8 // 2 == s + 9, turned, pack1)
    fzs[0] = pack0
    fzs[1] = pack1
    for k in (4, 5):
        start(fine_copy, k)

    gather_wait(1)
    xg[gx] = yg[...]
    gather_start(0)

    for k in (4, 5):
        arrived(fine_copy, k)
    p0 = fzr[0]
    p1 = fzr[1]
    for a in range(3):
        for j in range(8):
            s = 8 * a + j
            v = roll(e[a, j + 2, 0:8, :], -(FB + 2), 1)
            v = v + jnp.where(lane8 < 2, roll(p0, -(18 + 2 * s), 1), 0.0)
            v = v + jnp.where((lane8 >= 14) & (lane8 < 16), roll(p1, 14 - 2 * s, 1), 0.0)
            fine_out[a, j] = v[:, :16]

    gather_wait(0)
    for g in range(nx):
        for p in range(2):
            rows = xg[g, p].reshape(ky, 128)
            for a in range(3):
                coarse_out[a, 2 * g + p] = coarse_out[a, 2 * g + p] + rows[:, 32 * a : 32 * a + kz]

    for k in range(6):
        sent(halo, k)
    for k in range(2, 6):
        sent(fine_copy, k)
    for d in neighbours:
        pl.when(exists(d))(lambda d=d: coarse_copy(d).wait_send())
    for axis in range(3):
        for o in range(1, dims[axis]):
            gather_copy(axis, o).wait_send()


def per_device(dims, warped_image, fixed_image, fine_control, coarse_control):
    sx, sy, sz = warped_image.shape
    kx, ky, kz = coarse_control.shape[1:]
    nx, ny, nz = dims
    wide = max(dims)
    slabs = 19
    vmem = pl.BlockSpec(memory_space=pltpu.VMEM)
    hbm = pl.BlockSpec(memory_space=pl.ANY)
    v = lambda *shape: pltpu.VMEM(shape, F32)
    dma = pltpu.SemaphoreType.DMA
    return pl.pallas_call(
        lambda *refs: kernel(dims, *refs),
        out_shape=(
            jax.ShapeDtypeStruct(fine_control.shape, F32),
            jax.ShapeDtypeStruct(coarse_control.shape, F32),
        ),
        in_specs=[hbm, hbm, vmem, vmem, vmem, vmem, vmem],
        out_specs=(vmem, vmem),
        scratch_shapes=[
            v(sx, sy, sz), v(sx, sy, sz), v(sx + 4, sy + 16, sz),
            v(2, sx, 2, sz), v(2, sx, 2, sz), v(2, sy, 128), v(2, 2, sy, 128), v(2, sy, 128),
            v(sx, sy, sz), v(sy, 3 * slabs * 128), v(3, slabs, 24, 128), v(3, 12, 16, 128),
            v(3, 3, 2, 2, 128), v(27, 2, 2, 128), v(nz, 2, 2, 128), v(2, ny, 2, 128), v(nx, 2, ny, 2, 128),
            v(2, 3, 2, 16, 128), v(2, 24, 2, 128), v(2, 24, 2, 128), v(2, 8, 128), v(2, 8, 128), v(12, 16, 128),
            dma((2, 8)), dma((6,)), dma((6,)), dma((27,)), dma((27,)),
            dma((3, wide)), dma((3, wide)), dma((6,)), dma((6,)),
        ],
        compiler_params=pltpu.CompilerParams(collective_id=0, has_side_effects=True, vmem_limit_bytes=48 << 20),
        name="gradient",
    )(warped_image, fixed_image, fine_control, coarse_control,
      jnp.asarray(y_matrix(sy)), jnp.asarray(z_matrices(sz)), jnp.asarray(d_matrix(sz)))


def solution(mesh):
    dims = tuple(mesh.shape[a] for a in ("gx", "gy", "gz"))
    in_specs = (P("gx", "gy", "gz"), P("gx", "gy", "gz"), P(None, "gx", "gy", "gz"), P())
    out_specs = (P(None, "gx", "gy", "gz"), P())
    return jax.shard_map(
        lambda *args: per_device(dims, *args), mesh=mesh, in_specs=in_specs, out_specs=out_specs, check_vma=False
    )
```

profile of v0, /device:TPU:1, one launch (start us, length us, event | category | flops | bytes accessed | tf_op | source)
XLA Modules:
  0.0 54.5 jit_solution(15364906466509559208)
XLA Ops:
  0.6 0.0 copy-start
  0.6 1.6 %copy-done = f32[64,64,128]{2,1,0:T(8,128)S(1)} copy-done((f32[64,64,128]{2,1,0:T(8,128)S(1)}, f32[64,64,128]{2,1,0:T(8,128)}, u32[]{:S(2)}) %copy-start) | copy-done | bytes 2097176
  2.2 0.0 copy-start.1
  2.2 1.6 %copy-done.1 = f32[64,64,128]{2,1,0:T(8,128)S(1)} copy-done((f32[64,64,128]{2,1,0:T(8,128)S(1)}, f32[64,64,128]{2,1,0:T(8,128)}, u32[]{:S(2)}) %copy-start.1) | copy-done | bytes 2097176
  3.8 0.0 copy-start.2
  3.8 1.0 %copy-done.2 = f32[3,16,16,32]{3,2,1,0:T(8,128)S(1)} copy-done((f32[3,16,16,32]{3,2,1,0:T(8,128)S(1)}, f32[3,16,16,32]{3,2,1,0:T(8,128)}, u32[]{:S(2)}) %copy-start.2) | copy-done | bytes 98328
  4.8 0.0 copy-start.3
  4.8 1.0 %copy-done.3 = bf16[3,256,256]{2,1,0:T(8,128)(2,1)S(1)} copy-done((bf16[3,256,256]{2,1,0:T(8,128)(2,1)S(1)}, bf16[3,256,256]{2,1,0:T(8,128)(2,1)}, u32[]{:S(2)}) %copy-start.3) | copy-done | bytes 393240
  5.8 0.0 copy-start.4
  5.8 0.9 %copy-done.4 = f32[3,8,8,16]{3,2,1,0:T(8,128)S(1)} copy-done((f32[3,8,8,16]{3,2,1,0:T(8,128)S(1)}, f32[3,8,8,16]{3,2,1,0:T(8,128)}, u32[]{:S(2)}) %copy-start.4) | copy-done | bytes 12312
  6.7 0.0 copy-start.5
  6.7 0.8 %copy-done.5 = bf16[256,128]{1,0:T(8,128)(2,1)S(1)} copy-done((bf16[256,128]{1,0:T(8,128)(2,1)S(1)}, bf16[256,128]{1,0:T(8,128)(2,1)}, u32[]{:S(2)}) %copy-start.5) | copy-done | bytes 65560
  7.5 0.0 copy-start.6
  7.5 0.7 %copy-done.6 = bf16[48,128]{1,0:T(8,128)(2,1)S(1)} copy-done((bf16[48,128]{1,0:T(8,128)(2,1)S(1)}, bf16[48,128]{1,0:T(8,128)(2,1)}, u32[]{:S(2)}) %copy-start.6) | copy-done | bytes 12312
  8.2 44.8 %gradient.1 = (f32[3,8,8,16]{3,2,1,0:T(8,128)S(1)}, f32[3,16,16,32]{3,2,1,0:T(8,128)S(1)}) custom-call(f32[64,64,128]{2,1,0:T(8,128)S(1)} %copy-done, f32[64,64,128]{2,1,0:T(8,128)S(1)} %copy-done.1, f32[3,8,8,16]{3,2,1,0:T(8,128)S(1)} %copy-done.4, f32[3,16,16,32]{3,2,1,0:T(8,128)S(1)} %copy-done.2, bf16[48,128]{1,0:T(8,128)(2,1)S(1)} %copy-done.6, ...), custom_call_target="tpu_custom_call" | custom-call | tf_op jit(solution)/shard_map/gradient/pallas_call | solution.py:551
  53.1 0.6 %copy.11 = f32[3,8,8,16]{3,2,1,0:T(8,128)} copy(f32[3,8,8,16]{3,2,1,0:T(8,128)S(1)} %get-tuple-element.4) | data formatting | bytes 24576
  53.7 0.7 %copy.12 = f32[3,16,16,32]{3,2,1,0:T(8,128)} copy(f32[3,16,16,32]{3,2,1,0:T(8,128)S(1)} %get-tuple-element.5) | data formatting | bytes 196608
Async XLA Ops:
  0.6 1.6 %copy-start = (f32[64,64,128]{2,1,0:T(8,128)S(1)}, f32[64,64,128]{2,1,0:T(8,128)}, u32[]{:S(2)}) copy-start(f32[64,64,128]{2,1,0:T(8,128)} %refs_0_.1) | copy-start | bytes 6291460
  2.2 1.6 %copy-start.1 = (f32[64,64,128]{2,1,0:T(8,128)S(1)}, f32[64,64,128]{2,1,0:T(8,128)}, u32[]{:S(2)}) copy-start(f32[64,64,128]{2,1,0:T(8,128)} %refs_1_.1) | copy-start | bytes 6291460
  3.8 1.0 %copy-start.2 = (f32[3,16,16,32]{3,2,1,0:T(8,128)S(1)}, f32[3,16,16,32]{3,2,1,0:T(8,128)}, u32[]{:S(2)}) copy-start(f32[3,16,16,32]{3,2,1,0:T(8,128)} %refs_3_.1) | copy-start | bytes 294916
  4.8 1.0 %copy-start.3 = (bf16[3,256,256]{2,1,0:T(8,128)(2,1)S(1)}, bf16[3,256,256]{2,1,0:T(8,128)(2,1)}, u32[]{:S(2)}) copy-start(bf16[3,256,256]{2,1,0:T(8,128)(2,1)} %constant.7.clone.refs_5_) | copy-start | bytes 1179652
  5.8 0.9 %copy-start.4 = (f32[3,8,8,16]{3,2,1,0:T(8,128)S(1)}, f32[3,8,8,16]{3,2,1,0:T(8,128)}, u32[]{:S(2)}) copy-start(f32[3,8,8,16]{3,2,1,0:T(8,128)} %refs_2_.1) | copy-start | bytes 36868
  6.7 0.8 %copy-start.5 = (bf16[256,128]{1,0:T(8,128)(2,1)S(1)}, bf16[256,128]{1,0:T(8,128)(2,1)}, u32[]{:S(2)}) copy-start(bf16[256,128]{1,0:T(8,128)(2,1)} %constant.8.clone.refs_6_) | copy-start | bytes 196612
  7.5 0.7 %copy-start.6 = (bf16[48,128]{1,0:T(8,128)(2,1)S(1)}, bf16[48,128]{1,0:T(8,128)(2,1)}, u32[]{:S(2)}) copy-start(bf16[48,128]{1,0:T(8,128)(2,1)} %constant.6.clone.refs_4_) | copy-start | bytes 36868
where the time goes:
time: 54.9 us; the launch traced here: 54.5 us
  Pallas kernels  44.8 us (82%)
  local copies, waits for them, and re-layouts  8.99 us (16%)
  between operations  0.65 us (1%)
    pallas_call x1, Pallas kernels, per_device(): pl.pallas_call(lambda *refs: kernel(dims, *refs), out_shape=(jax.ShapeDty...  44.8 us
    unnamed x16, local copies, waits for them, and re-layouts  8.99 us

commit v1 on v0

v1 whole, which is shorter than its diff:
```python
import itertools

import jax
import jax.numpy as jnp
import numpy as np
from jax import lax
from jax.experimental import pallas as pl
from jax.experimental.pallas import tpu as pltpu
from jax.sharding import PartitionSpec as P

SPF = 8
SPC = 32
BEND = 0.01
FB = 0
MESH = pl.DeviceIdType.MESH
F32 = jnp.float32
BF16 = jnp.bfloat16


def beta(t):
    m = np.abs(t)
    r = 2.0 - m
    return np.where(m < 1.0, 2.0 / 3.0 - m * m + 0.5 * m**3, np.where(m < 2.0, r**3 / 6.0, 0.0))


def basis(voxels, points, spacing, first):
    v = np.arange(voxels)[:, None] + 0.5
    c = (np.arange(points)[None, :] + first) * spacing + 0.5 * spacing
    return beta((v - c) / spacing)


def halves(w):
    hi = np.asarray(w, np.float32).astype(jnp.bfloat16)
    lo = (np.asarray(w, np.float64) - hi.astype(np.float64)).astype(np.float32).astype(jnp.bfloat16)
    return hi, lo


W4 = beta((np.arange(4)[:, None] + 4.5 - 4.0 * np.arange(4)[None, :]) / 4.0) / 24.0
TWO = np.array([1.0, 4.0, 6.0, 4.0, 1.0]) / 8.0


def spread(c, step):
    out = np.zeros((len(c) - 1) * step + 1)
    out[::step] = c
    return out


C29 = np.convolve(np.convolve(TWO, spread(TWO, 2)), spread(TWO, 4))


def y_matrix(sy):
    rows = np.zeros((24, sy))
    rows[:12] = basis(sy, 12, SPF, -2).T * SPF**-1.5
    rows[16:22] = basis(sy, 6, SPC, -2).T * SPC**-1.5
    hi, lo = halves(rows)
    return np.concatenate([np.concatenate([hi, hi], 1), np.concatenate([lo, lo], 1)], 0)


def stacked(cols):
    hi, lo = halves(cols)
    half = np.concatenate([hi, lo], 1)
    return np.concatenate([half, half], 0)


def z_matrices(sz):
    fine = np.zeros((sz, 128))
    fine[:, FB : FB + 20] = basis(sz, 20, SPF, -2)
    out = [stacked(fine)]
    for a in range(3):
        cols = np.zeros((sz, 128))
        for piece in range(4):
            first = 32 * piece + 8 * a
            cols[:, first : first + 8] = basis(sz, 8, SPC, -2)
        out.append(stacked(cols))
    return np.stack(out)


def d_matrix(sz):
    d = np.zeros((sz, sz), np.float32)
    for shift, value in ((-2, 1.0), (-1, -8.0), (1, 8.0), (2, -1.0)):
        for v in range(sz):
            if 0 <= v + shift < sz:
                d[v + shift, v] = value
    return np.concatenate([d, d], 0).astype(jnp.bfloat16)


def h_matrix(sz):
    h = np.zeros((128, sz), np.float32)
    for lane in range(128):
        h[lane, (sz - 2, sz - 1, 0, 1)[lane % 4]] = 1.0
    return np.concatenate([h, h], 0).astype(jnp.bfloat16)


def split(x):
    hi = x.astype(BF16)
    return hi, (x - hi.astype(F32)).astype(BF16)


def lanes(shape):
    return lax.broadcasted_iota(jnp.int32, shape, len(shape) - 1)


def roll(x, shift, axis):
    return pltpu.roll(x, shift % x.shape[axis] if isinstance(shift, int) else shift, axis)


class Place:
    def __init__(self, dims):
        self.dims = dims
        self.pos = tuple(lax.axis_index(a) for a in ("gx", "gy", "gz"))
        self.has = [{-1: p > 0, 1: p < n - 1} for p, n in zip(self.pos, dims)]

    def exists(self, d):
        cond = None
        for i in range(3):
            if d[i]:
                one = self.has[i][d[i]]
                cond = one if cond is None else jnp.logical_and(cond, one)
        return cond

    def at(self, d):
        return tuple(self.pos[i] + d[i] for i in range(3))

    def ring(self, axis, o):
        t = lax.rem(self.pos[axis] + o, self.dims[axis])
        return tuple(t if i == axis else self.pos[i] for i in range(3)), t

    def seen(self, dx, dy):
        return self.exists((dx, dy, 0))

    def if_seen(self, dx, dy, fn):
        if dx or dy:
            pl.when(self.seen(dx, dy))(fn)
        else:
            fn()

    def beside(self, dx, dy, o):
        gx, gy, gz = self.pos
        return (gx + dx, gy + dy, lax.rem(gz + o, self.dims[2]))

    def start(self, make, k):
        d, copy = make(k)
        pl.when(self.exists(d))(lambda: copy.start())

    def sent(self, make, k):
        d, copy = make(k)
        pl.when(self.exists(d))(lambda: copy.wait_send())

    def arrived(self, make, k):
        d, copy = make(k)
        pl.when(self.exists([-v for v in d]))(lambda: copy.wait_recv())


def ring_order(n):
    return sorted(range(n), key=lambda o: -min(o, n - o))


SIDES = list(itertools.product((-1, 0, 1), repeat=2))


def layers(dims, w_hbm, f_hbm, ctl_h, dz_h, sp, diff, dzb, cz, e,
           ctl, dz_w, small_sem, wb, fb, hys, hyr, hzs, hzr, fw, img_sem, hs, hr):
    nx, ny, nz = dims
    here = Place(dims)
    pos = here.pos
    gx, gy, gz = pos
    has, exists, at, ring, seen, if_seen, beside = (
        here.has, here.exists, here.at, here.ring, here.seen, here.if_seen, here.beside)
    start, sent, arrived = here.start, here.sent, here.arrived
    sides = SIDES
    zero8 = jnp.zeros((8, 128), F32)
    lane64 = lanes((64, 128))

    bar = pltpu.get_barrier_semaphore()
    count = 0
    for axis in range(3):
        for side in (-1, 1):
            d = tuple(side if i == axis else 0 for i in range(3))
            pl.when(exists(d))(lambda d=d: pl.semaphore_signal(bar, inc=1, device_id=at(d), device_id_type=MESH))
            count = count + has[axis][side].astype(jnp.int32)

    chunks = 8
    planes = 8
    for c in range(chunks):
        part = pl.ds(c * planes, planes)
        pltpu.make_async_copy(w_hbm.at[part], wb.at[part], img_sem.at[0, c]).start()
        pltpu.make_async_copy(f_hbm.at[part], fb.at[part], img_sem.at[1, c]).start()
    small = [pltpu.make_async_copy(dz_h, dz_w, small_sem.at[0]), pltpu.make_async_copy(ctl_h, ctl, small_sem.at[1])]
    for copy in small:
        copy.start()

    for side, d in ((0, -1), (1, 1)):
        @pl.when(jnp.logical_not(has[0][d]))
        def _(side=side):
            sp[66 * side : 66 * side + 2, 8:72, :] = jnp.zeros((2, 64, 128), F32)

        @pl.when(jnp.logical_not(has[1][d]))
        def _(side=side):
            hyr[side] = jnp.zeros(hyr.shape[1:], F32)

        @pl.when(jnp.logical_not(has[2][d]))
        def _(side=side):
            hzr[side] = jnp.zeros(hzr.shape[1:], F32)

    hzs[...] = jnp.zeros(hzs.shape, F32)


    def sum_chunk(c, _):
        base = pl.multiple_of(c * planes, planes)
        part = pl.ds(base, planes)
        pltpu.make_async_copy(w_hbm.at[part], wb.at[part], img_sem.at[0, c]).wait()
        pltpu.make_async_copy(f_hbm.at[part], fb.at[part], img_sem.at[1, c]).wait()
        h = c // 4
        group = lane64 // 4 - 8 * lax.rem(c, 4)
        packed = hzs[h]
        for j in range(planes):
            w = wb[base + j]
            f = fb[base + j]
            s = w + f
            diff[base + j] = w - f
            sp[base + j + 2, 8:72, :] = s
            hys[0, base + j] = s[0:2]
            hys[1, base + j] = s[62:64]
            turned = pltpu.roll(s, 32 * lax.rem(c, 4) + 4 * j + 2, 1)
            packed = jnp.where(group == j, turned, packed)
        hzs[h] = packed
        return 0

    lax.fori_loop(0, chunks, sum_chunk, 0)
    pl.semaphore_wait(bar, count)

    def halo(k):
        axis, side = k // 2, k % 2
        d = [0, 0, 0]
        d[axis] = 2 * side - 1
        if axis == 0:
            src = sp.at[pl.ds(2 if side == 0 else 64, 2), pl.ds(8, 64), :]
            dst = sp.at[pl.ds(66 if side == 0 else 0, 2), pl.ds(8, 64), :]
        elif axis == 1:
            src, dst = hys.at[side], hyr.at[1 - side]
        else:
            src, dst = hzs, hzr.at[1 - side]
        return d, pltpu.make_async_remote_copy(
            src_ref=src, dst_ref=dst, send_sem=hs.at[k], recv_sem=hr.at[k],
            device_id=at(d), device_id_type=MESH)

    for k in (4, 5, 2, 3, 0, 1):
        start(halo, k)

    small[0].wait()

    def dz_chunk(c, _):
        base = pl.multiple_of(c * 16, 16)
        for half in range(2):
            parts = [jnp.concatenate(split(sp[base + 8 * half + j + 2, 8:72, :]), 1) for j in range(8)]
            out = jnp.dot(jnp.concatenate(parts, 0), dz_w[...], preferred_element_type=F32)
            for j in range(8):
                dzb[base + 8 * half + j] = out[64 * j : 64 * (j + 1)]
        return 0

    lax.fori_loop(0, 4, dz_chunk, 0)

    small[1].wait()

    row16 = lax.broadcasted_iota(jnp.int32, (16, 128), 0)
    lane16 = lanes((16, 128))
    row_g = row16 - 2 + gy * 8
    lane_g = lane16 - (FB + 2) + gz * 16
    in_grid = (row_g >= 0) & (row_g < ny * 8) & (lane_g >= 0) & (lane_g < nz * 16)

    def lap(centre, low, high):
        total = roll(centre, 1, 0) + roll(centre, -1, 0) + roll(centre, 1, 1) + roll(centre, -1, 1)
        if low is not None:
            total = total + low
        if high is not None:
            total = total + high
        return total - 6.0 * centre

    def fine_bend(a, _):
        for j in range(8):
            block = jnp.concatenate([ctl[a, j], jnp.zeros((8, 112), F32)], 1)
            block = jnp.concatenate([block, zero8], 0)
            fw[j + 2] = roll(roll(block, 2, 0), FB + 2, 1)
        zero16 = jnp.zeros((16, 128), F32)
        for j in (0, 1, 10, 11):
            fw[j] = zero16
        first = []
        for j in range(12):
            if j in (0, 11):
                first.append(None)
                continue
            low = fw[j - 1] if 0 < j else None
            high = fw[j + 1] if j < 11 else None
            value = lap(fw[j], low, high)
            p = gx * 8 + j - 2
            ok = in_grid & (p >= 0) & (p < nx * 8)
            first.append(jnp.where(ok, value, 0.0))
        for j in range(12):
            centre = first[j] if first[j] is not None else zero16
            low = first[j - 1] if j > 0 else None
            high = first[j + 1] if j < 11 else None
            e[a, j] = BEND * lap(centre, low, high)
        return 0

    lax.fori_loop(0, 3, fine_bend, 0)

    for k in range(6):
        arrived(halo, k)

    def place_y(x, _):
        sp[x + 2, 6:8, :] = hyr[0, x]
        sp[x + 2, 72:74, :] = hyr[1, x]
        return 0

    lax.fori_loop(0, 64, place_y, 0, unroll=8)

    m4 = lane64 % 4
    for h in range(2):
        u = jnp.where(m4 < 2, hzr[0, h], hzr[1, h])
        a_part = jnp.where(m4 < 2, -roll(u, -2, 1), roll(u, 2, 1))
        b_part = jnp.where(m4 == 1, 8.0 * roll(u, -1, 1), jnp.where(m4 == 2, -8.0 * roll(u, 1, 1), 0.0))
        cz[h] = a_part + b_part
    for k in range(6):
        sent(halo, k)


def gradient(dims, sp, diff, dzb, cz, e0, cctl_h, wy_h, wz_h, h_h, fine_out, coarse_out,
             cctl, wy, wz, h_w, small_sem, dz2, xs, zs, e, csend, crecv, yg, xg, mix,
             fxr, fys, fyr, fzs, fzr, cs, cr, gs, gr, fs, fr):
    nx, ny, nz = dims
    here = Place(dims)
    pos = here.pos
    gx, gy, gz = pos
    has, exists, at, ring, seen, if_seen, beside = (
        here.has, here.exists, here.at, here.ring, here.seen, here.if_seen, here.beside)
    start, sent, arrived = here.start, here.sent, here.arrived
    sides = SIDES
    zero8 = jnp.zeros((8, 128), F32)
    lane64 = lanes((64, 128))

    small = [pltpu.make_async_copy(src, dst, small_sem.at[i]) for i, (src, dst) in enumerate(
        ((h_h, h_w), (wy_h, wy), (wz_h, wz), (cctl_h, cctl)))]
    for copy in small:
        copy.start()

    bar = pltpu.get_barrier_semaphore()
    for dx, dy in sides:
        def greet(dx=dx, dy=dy):
            for o in ring_order(nz):
                if dx or dy or o:
                    pl.semaphore_signal(bar, inc=1, device_id=beside(dx, dy, o), device_id_type=MESH)
        if_seen(dx, dy, greet)
    for axis in range(2):
        for o in range(2, dims[axis] - 1):
            device, t = ring(axis, o)
            pl.when(jnp.abs(t - pos[axis]) > 1)(lambda device=device: pl.semaphore_signal(
                bar, inc=1, device_id=device, device_id_type=MESH))
        for o in (1, dims[axis] - 1):
            device, t = ring(axis, o)
            pl.when(jnp.abs(t - pos[axis]) > 1)(lambda device=device: pl.semaphore_signal(
                bar, inc=1, device_id=device, device_id_type=MESH))
    wide = [1 + h[-1].astype(jnp.int32) + h[1].astype(jnp.int32) for h in has]
    greeted = wide[0] * wide[1] * nz - 1 + (nx - wide[0]) + (ny - wide[1])

    for side, d in ((0, -1), (1, 1)):
        for axis, ref in enumerate((fxr, fyr, fzr)):
            @pl.when(jnp.logical_not(has[axis][d]))
            def _(side=side, ref=ref):
                ref[side] = jnp.zeros(ref.shape[1:], F32)
    for dx, dy in sides:
        if dx or dy:
            @pl.when(jnp.logical_not(seen(-dx, -dy)))
            def _(dx=dx, dy=dy):
                crecv[3 * (dx + 1) + dy + 1] = zero8

    def fine_copy(k):
        axis, side = k // 2, k % 2
        d = [0, 0, 0]
        d[axis] = 2 * side - 1
        if axis == 0:
            src, dst = e.at[:, pl.ds(10 * side, 2)], fxr.at[1 - side]
        elif axis == 1:
            src, dst = fys.at[side], fyr.at[1 - side]
        else:
            src, dst = fzs.at[side], fzr.at[1 - side]
        return d, pltpu.make_async_remote_copy(
            src_ref=src, dst_ref=dst, send_sem=fs.at[k], recv_sem=fr.at[k],
            device_id=at(d), device_id_type=MESH)

    small[0].wait()

    def z_fix(c, _):
        base = pl.multiple_of(c * 16, 16)
        layer = cz[c // 2]
        for half in range(2):
            group = lane64 // 4 - 16 * lax.rem(c, 2) - 8 * half
            parts = [jnp.concatenate(split(jnp.where(group == j, layer, 0.0)), 1) for j in range(8)]
            out = jnp.dot(jnp.concatenate(parts, 0), h_w[...], preferred_element_type=F32)
            for j in range(8):
                dz2[base + 8 * half + j] = dzb[base + 8 * half + j] + out[64 * j : 64 * (j + 1)]
        return 0

    lax.fori_loop(0, 4, z_fix, 0)

    groups = 16
    slabs = groups + 3

    def column(yt, _):
        r0 = pl.multiple_of(8 * yt, 8)

        def put(a, g, value):
            xs[pl.ds(r0, 8), pl.ds(pl.multiple_of((a * slabs + g) * 128, 128), 128)] = value

        def pair(gg, acc):
            acc = [list(row) for row in acc]
            x0 = 8 * gg
            c = [sp[x0 + i, pl.ds(r0 + 8, 8), :] for i in range(12)]
            for sub in range(2):
                for k in range(4):
                    i = 4 * sub + k
                    plane = x0 + i + 2
                    sx = (c[i] - c[i + 4]) + 8.0 * (c[i + 3] - c[i + 1])
                    ym2 = sp[plane, pl.ds(r0 + 6, 8), :]
                    ym1 = sp[plane, pl.ds(r0 + 7, 8), :]
                    yp1 = sp[plane, pl.ds(r0 + 9, 8), :]
                    yp2 = sp[plane, pl.ds(r0 + 10, 8), :]
                    sy = (ym2 - yp2) + 8.0 * (yp1 - ym1)
                    sz = dz2[x0 + i, pl.ds(r0, 8), :]
                    dv = diff[x0 + i, pl.ds(r0, 8), :]
                    for a, s in enumerate((sx, sy, sz)):
                        f = dv * s
                        for m in range(4):
                            acc[a][m] = acc[a][m] + float(W4[k, m]) * f
                for a in range(3):
                    put(a, 2 * gg + sub, acc[a][0])
                    acc[a] = [acc[a][1], acc[a][2], acc[a][3], jnp.zeros((8, 128), F32)]
            return tuple(tuple(row) for row in acc)

        acc = lax.fori_loop(0, groups // 2, pair, tuple(tuple(zero8 for _ in range(4)) for _ in range(3)))
        for a in range(3):
            for m in range(3):
                put(a, groups + m, acc[a][m])
        return 0

    lax.fori_loop(0, 8, column, 0)

    for copy in small[1:]:
        copy.wait()
    total = None
    for a in range(3):
        x = xs[:, a * slabs * 128 : (a + 1) * slabs * 128]
        hi, lo = split(x)
        y = jnp.dot(wy[...], jnp.concatenate([hi, lo], 0), preferred_element_type=F32)
        y = y[:24] + y[24:]
        pieces = [y[:, 128 * i : 128 * (i + 1)] for i in range(slabs)]
        hi, lo = split(jnp.concatenate([p[16:24] for p in pieces], 0))
        z = jnp.dot(jnp.concatenate([hi, lo], 1), wz[1 + a], preferred_element_type=F32)
        z = z[:, :128] + z[:, 128:]
        total = z if total is None else total + z
        hi, lo = split(jnp.concatenate([p[:16] for p in pieces], 0))
        z = jnp.dot(jnp.concatenate([hi, lo], 1), wz[0], preferred_element_type=F32)
        z = z[:, :128] + z[:, 128:]
        for i in range(slabs):
            zs[a, i] = z[16 * i : 16 * (i + 1)]

    lane8 = lanes((8, 128))
    taken = []
    for jj in range(6):
        v = None
        for i in range(slabs):
            tap = i - 8 * jj + 25
            if 0 <= tap < 29:
                term = float(C29[tap]) * total[8 * i : 8 * (i + 1)]
                v = term if v is None else v + term
        taken.append(v)
    for g in range(3):
        v = jnp.where(lane8 < 64, taken[2 * g], taken[2 * g + 1])
        csend[g] = jnp.where(lane8 // 32 % 2 == 0, v, roll(v, -1, 0))
    crecv[4, pl.ds(gz, 1), :] = csend[1, 2:3, :]

    def coarse_copy(dx, dy, o):
        slot = 3 * (dx + 1) + dy + 1
        return pltpu.make_async_remote_copy(
            src_ref=csend.at[dx + 1, pl.ds(2 * (dy + 1), 1), :], dst_ref=crecv.at[slot, pl.ds(gz, 1), :],
            send_sem=cs.at[slot, o], recv_sem=cr.at[slot, o], device_id=beside(dx, dy, o), device_id_type=MESH)

    def coarse_arrival(dx, dy, o):
        slot = 3 * (dx + 1) + dy + 1
        s = lax.rem(gz + nz - o, nz)
        return pltpu.make_async_remote_copy(
            src_ref=csend.at[dx + 1, pl.ds(2 * (dy + 1), 1), :], dst_ref=crecv.at[slot, pl.ds(s, 1), :],
            send_sem=cs.at[slot, o], recv_sem=cr.at[slot, o], device_id=beside(dx, dy, o), device_id_type=MESH)

    def coarse_all(fn):
        for o in ring_order(nz):
            for dx, dy in sorted(sides, key=lambda d: -abs(d[0]) - abs(d[1])):
                if o or dx or dy:
                    fn(dx, dy, o)

    pl.semaphore_wait(bar, greeted)
    coarse_all(lambda dx, dy, o: if_seen(dx, dy, lambda: coarse_copy(dx, dy, o).start()))

    for a in range(3):
        for j in range(12):
            v = e0[a, j]
            for k in range(5):
                i = 2 * j - 4 + k
                if 0 <= i < slabs:
                    v = v + float(TWO[k]) * zs[a, i]
            e[a, j] = v
    for k in (0, 1):
        start(fine_copy, k)

    coarse_all(lambda dx, dy, o: if_seen(-dx, -dy, lambda: coarse_arrival(dx, dy, o).wait_recv()))
    line = crecv[0]
    for i in range(1, 9):
        line = line + crecv[i]
    line = pltpu.roll(line, 0, 1, stride=4, stride_axis=0)
    place = lane8 % 32 + 2 - 4 * lax.broadcasted_iota(jnp.int32, (8, 128), 0)
    for a in range(3):
        piece = jnp.where((place >= 0) & (place < 8), roll(line, -2 - 8 * a, 1), 0.0)
        yg[a, pl.ds(gy, 1), :] = jnp.sum(piece, axis=0, keepdims=True)

    def gather_copy(axis, o):
        device, _ = ring(axis, o)
        if axis == 1:
            src = dst = yg.at[:, pl.ds(gy, 1), :]
        else:
            src, dst = yg, xg.at[gx]
        return pltpu.make_async_remote_copy(
            src_ref=src, dst_ref=dst, send_sem=gs.at[axis, o], recv_sem=gr.at[axis, o],
            device_id=device, device_id_type=MESH)

    def offsets(axis):
        return ring_order(dims[axis])[:-1]

    def gather_start(axis):
        for o in offsets(axis):
            gather_copy(axis, o).start()

    def gather_wait(axis):
        n = dims[axis]
        for o in reversed(offsets(axis)):
            s = lax.rem(pos[axis] + n - o, n)
            dst = (xg.at[s], yg.at[:, pl.ds(s, 1), :])[axis]
            src = yg if axis == 0 else dst
            pltpu.make_async_remote_copy(
                src_ref=src, dst_ref=dst, send_sem=gs.at[axis, o], recv_sem=gr.at[axis, o],
                device_id=ring(axis, o)[0], device_id_type=MESH).wait_recv()

    gather_start(1)

    kx, ky, kz = cctl.shape[1:]
    shape = (ky, kz)
    crow = lax.broadcasted_iota(jnp.int32, (ky, 128), 0)
    clane = lanes((ky, 128))

    def clap(centre, low, high):
        total = jnp.where(crow > 0, roll(centre, 1, 0), 0.0) + jnp.where(crow < ky - 1, roll(centre, -1, 0), 0.0)
        total = total + roll(centre, 1, 1) + roll(centre, -1, 1)
        if low is not None:
            total = total + low
        if high is not None:
            total = total + high
        return jnp.where(clane < kz, total - 6.0 * centre, 0.0)

    def coarse_bend(a, _):
        field = [jnp.concatenate([cctl[a, j], jnp.zeros((ky, 128 - kz), F32)], 1) for j in range(kx)]
        for _level in range(2):
            field = [clap(field[j], field[j - 1] if j else None, field[j + 1] if j < kx - 1 else None)
                     for j in range(kx)]
        for j in range(kx):
            coarse_out[a, j] = BEND * field[j][:, :kz]
        return 0

    lax.fori_loop(0, 3, coarse_bend, 0)

    for k in (0, 1):
        sent(fine_copy, k)
        arrived(fine_copy, k)
    for a in range(3):
        for j in range(8):
            v = e[a, j + 2]
            if j < 2:
                v = v + fxr[0, a, j]
            if j >= 6:
                v = v + fxr[1, a, j - 6]
            e[a, j + 2] = v
            fys[0, 8 * a + j] = v[0:2]
            fys[1, 8 * a + j] = v[10:12]
    for k in (2, 3):
        start(fine_copy, k)

    gather_wait(1)
    xg[gx] = yg[...]
    gather_start(0)

    for k in (2, 3):
        arrived(fine_copy, k)
    pack0 = zero8
    pack1 = zero8
    zero4 = jnp.zeros((4, 128), F32)
    for a in range(3):
        for j in range(8):
            s = 8 * a + j
            v = e[a, j + 2]
            edges = jnp.concatenate([fyr[0, s], zero4, fyr[1, s]], 0)
            v = roll(v, -2, 0)[0:8] + edges
            e[a, j + 2, 0:8, :] = v
            turned = roll(v, 2 * s - FB, 1)
            pack0 = jnp.where(lane8 // 2 == s, turned, pack0)
            pack1 = jnp.where(lane8 // 2 == s + 9, turned, pack1)
    fzs[0] = pack0
    fzs[1] = pack1
    for k in (4, 5):
        start(fine_copy, k)

    for k in (4, 5):
        arrived(fine_copy, k)
    p0 = fzr[0]
    p1 = fzr[1]
    for a in range(3):
        for j in range(8):
            s = 8 * a + j
            v = roll(e[a, j + 2, 0:8, :], -(FB + 2), 1)
            v = v + jnp.where(lane8 < 2, roll(p0, -(18 + 2 * s), 1), 0.0)
            v = v + jnp.where((lane8 >= 14) & (lane8 < 16), roll(p1, 14 - 2 * s, 1), 0.0)
            fine_out[a, j] = v[:, :16]

    gather_wait(0)
    for g in range(nx):
        for a in range(3):
            rows = xg[g, a]
            for p in range(2):
                for q in range(2):
                    mix[a, 2 * g + p, pl.ds(q, ny, stride=2), :] = roll(rows, -(64 * p + 32 * q), 1)
    for a in range(3):
        for j in range(kx):
            coarse_out[a, j] = coarse_out[a, j] + mix[a, j][:, :kz]

    for k in range(2, 6):
        sent(fine_copy, k)
    coarse_all(lambda dx, dy, o: if_seen(dx, dy, lambda: coarse_copy(dx, dy, o).wait_send()))
    for axis in range(2):
        for o in range(1, dims[axis]):
            gather_copy(axis, o).wait_send()


def per_device(dims, warped_image, fixed_image, fine_control, coarse_control):
    sx, sy, sz = warped_image.shape
    kx, ky, kz = coarse_control.shape[1:]
    nx, ny, nz = dims
    wide = max(dims)
    slabs = 19
    vmem = pl.BlockSpec(memory_space=pltpu.VMEM)
    hbm = pl.BlockSpec(memory_space=pltpu.HBM)
    v = lambda *shape: pltpu.VMEM(shape, F32)
    h = lambda *shape: pltpu.VMEM(shape, BF16)
    out = lambda *shape: jax.ShapeDtypeStruct(shape, F32)
    dma = pltpu.SemaphoreType.DMA
    far = lambda x: pltpu.with_memory_space_constraint(jnp.asarray(x), pltpu.HBM)
    local = pl.pallas_call(
        lambda *refs: layers(dims, *refs),
        out_shape=(out(sx + 4, sy + 16, sz), out(sx, sy, sz), out(sx, sy, sz), out(2, sy, 128), out(3, 12, 16, 128)),
        in_specs=[hbm] * 4,
        out_specs=(vmem,) * 5,
        scratch_shapes=[
            v(*fine_control.shape), h(2 * sz, sz), dma((2,)), v(sx, sy, sz), v(sx, sy, sz),
            v(2, sx, 2, sz), v(2, sx, 2, sz), v(2, sy, 128), v(2, 2, sy, 128), v(12, 16, 128),
            dma((2, 8)), dma((6,)), dma((6,)),
        ],
        compiler_params=pltpu.CompilerParams(collective_id=0, has_side_effects=True, vmem_limit_bytes=24 << 20),
        name="layers",
    )(far(warped_image), far(fixed_image), far(fine_control), far(d_matrix(sz)))
    return pl.pallas_call(
        lambda *refs: gradient(dims, *refs),
        out_shape=(out(*fine_control.shape), out(*coarse_control.shape)),
        in_specs=[vmem] * 5 + [hbm] * 4,
        out_specs=(vmem, vmem),
        scratch_shapes=[
            v(*coarse_control.shape), h(48, 2 * sy), h(4, 2 * sz, 256), h(256, sz), dma((4,)),
            v(sx, sy, sz), v(sy, 3 * slabs * 128), v(3, slabs, 16, 128), v(3, 12, 16, 128),
            v(3, 8, 128), v(9, nz, 128), v(3, ny, 128), v(nx, 3, ny, 128), v(3, kx, ky, 128),
            v(2, 3, 2, 16, 128), v(2, 24, 2, 128), v(2, 24, 2, 128), v(2, 8, 128), v(2, 8, 128),
            dma((9, nz)), dma((9, nz)), dma((2, wide)), dma((2, wide)), dma((6,)), dma((6,)),
        ],
        compiler_params=pltpu.CompilerParams(collective_id=1, has_side_effects=True, vmem_limit_bytes=24 << 20),
        name="gradient",
    )(*local, far(coarse_control), far(y_matrix(sy)), far(z_matrices(sz)), far(h_matrix(sz)))


def solution(mesh):
    dims = tuple(mesh.shape[a] for a in ("gx", "gy", "gz"))
    in_specs = (P("gx", "gy", "gz"), P("gx", "gy", "gz"), P(None, "gx", "gy", "gz"), P())
    out_specs = (P(None, "gx", "gy", "gz"), P())
    return jax.shard_map(
        lambda *args: per_device(dims, *args), mesh=mesh, in_specs=in_specs, out_specs=out_specs, check_vma=False
    )
```

time: 54.9 us -> 43.7 us (0.80)
  local copies, waits for them, and re-layouts: 8.99 us -> 1.39 us
  Pallas kernels: 44.8 us -> 41.4 us
    unnamed x16 -> x2, local copies, waits for them, and re-layouts: 8.99 us -> 1.39 us
    pallas_call x1 -> x2, Pallas kernels: 44.8 us -> 41.4 us  [the longest x1 30.2 us: per_device(): pl.pallas_call(lambda *refs: gradient(dims, *refs), out_shape=(out(*fine_...]
where the time goes in v1:
time: 43.7 us; the launch traced here: 43.5 us
  Pallas kernels  41.4 us (95%)
  local copies, waits for them, and re-layouts  1.39 us (3%)
  between operations  0.65 us (1%)
    pallas_call x1, Pallas kernels, per_device(): pl.pallas_call(lambda *refs: gradient(dims, *refs), out_shape=(out(*fine_...  30.2 us
    pallas_call x1, Pallas kernels, per_device(): pl.pallas_call(lambda *refs: layers(dims, *refs), out_shape=(out(sx + 4,...  11.2 us
    unnamed x2, local copies, waits for them, and re-layouts  1.39 us

profile of v1, /device:TPU:1, one launch (start us, length us, event | category | flops | bytes accessed | tf_op | source)
XLA Modules:
  0.0 43.5 jit_solution(8472776155520507183)
XLA Ops:
  0.6 11.2 %layers.1 = (f32[68,80,128]{2,1,0:T(8,128)S(1)}, f32[64,64,128]{2,1,0:T(8,128)S(1)}, f32[64,64,128]{2,1,0:T(8,128)S(1)}, f32[2,64,128]{2,1,0:T(8,128)S(1)}, f32[3,12,16,128]{3,2,1,0:T(8,128)S(1)}) custom-call(f32[64,64,128]{2,1,0:T(8,128)} %refs_0_.1, f32[64,64,128]{2,1,0:T(8,128)} %refs_1_.1, f32[3,8,8,16]{3,2,1,0:T(8,128)} %refs_2_.1, ...), custom_call_target="tpu_custom_call" | custom-call | tf_op jit(solution)/shard_map/layers/pallas_call | solution.py:662
  11.8 30.2 %gradient.1 = (f32[3,8,8,16]{3,2,1,0:T(8,128)S(1)}, f32[3,16,16,32]{3,2,1,0:T(8,128)S(1)}) custom-call(f32[68,80,128]{2,1,0:T(8,128)S(1)} %get-tuple-element.7.refs_0_, f32[64,64,128]{2,1,0:T(8,128)S(1)} %get-tuple-element.8.refs_1_, f32[64,64,128]{2,1,0:T(8,128)S(1)} %get-tuple-element.9.refs_2_, f32[2,64,128]{2,1,0:T(8,128)S(1)} %get-tuple-element.10.refs_3_, ...), custom_call_target="tpu_custom_call" | custom-call | tf_op jit(solution)/shard_map/gradient/pallas_call | solution.py:675
  42.1 0.6 %copy.12 = f32[3,8,8,16]{3,2,1,0:T(8,128)} copy(f32[3,8,8,16]{3,2,1,0:T(8,128)S(1)} %get-tuple-element.14) | data formatting | bytes 24576
  42.7 0.7 %copy.13 = f32[3,16,16,32]{3,2,1,0:T(8,128)} copy(f32[3,16,16,32]{3,2,1,0:T(8,128)S(1)} %get-tuple-element.15) | data formatting | bytes 196608

commit v2 on v1

--- a/solution.py
+++ b/solution.py
@@ -179,8 +179,8 @@
             pl.when(exists(d))(lambda d=d: pl.semaphore_signal(bar, inc=1, device_id=at(d), device_id_type=MESH))
             count = count + has[axis][side].astype(jnp.int32)
 
-    chunks = 8
-    planes = 8
+    chunks = 4
+    planes = 16
     for c in range(chunks):
         part = pl.ds(c * planes, planes)
         pltpu.make_async_copy(w_hbm.at[part], wb.at[part], img_sem.at[0, c]).start()
@@ -203,31 +203,6 @@
             hzr[side] = jnp.zeros(hzr.shape[1:], F32)
 
     hzs[...] = jnp.zeros(hzs.shape, F32)
-
-
-    def sum_chunk(c, _):
-        base = pl.multiple_of(c * planes, planes)
-        part = pl.ds(base, planes)
-        pltpu.make_async_copy(w_hbm.at[part], wb.at[part], img_sem.at[0, c]).wait()
-        pltpu.make_async_copy(f_hbm.at[part], fb.at[part], img_sem.at[1, c]).wait()
-        h = c // 4
-        group = lane64 // 4 - 8 * lax.rem(c, 4)
-        packed = hzs[h]
-        for j in range(planes):
-            w = wb[base + j]
-            f = fb[base + j]
-            s = w + f
-            diff[base + j] = w - f
-            sp[base + j + 2, 8:72, :] = s
-            hys[0, base + j] = s[0:2]
-            hys[1, base + j] = s[62:64]
-            turned = pltpu.roll(s, 32 * lax.rem(c, 4) + 4 * j + 2, 1)
-            packed = jnp.where(group == j, turned, packed)
-        hzs[h] = packed
-        return 0
-
-    lax.fori_loop(0, chunks, sum_chunk, 0)
-    pl.semaphore_wait(bar, count)
 
     def halo(k):
         axis, side = k // 2, k % 2
@@ -244,8 +219,61 @@
             src_ref=src, dst_ref=dst, send_sem=hs.at[k], recv_sem=hr.at[k],
             device_id=at(d), device_id_type=MESH)
 
-    for k in (4, 5, 2, 3, 0, 1):
-        start(halo, k)
+    def part_of(k, c):
+        axis, side = k // 2, k % 2
+        if axis == 0:
+            return halo(k)
+        d = [0, 0, 0]
+        d[axis] = 2 * side - 1
+        if axis == 1:
+            part = pl.ds(c * planes, planes)
+            src, dst = hys.at[side, part], hyr.at[1 - side, part]
+        else:
+            src, dst = hzs.at[c // 2], hzr.at[1 - side, c // 2]
+        return d, pltpu.make_async_remote_copy(
+            src_ref=src, dst_ref=dst, send_sem=hs.at[k], recv_sem=hr.at[k],
+            device_id=at(d), device_id_type=MESH)
+
+    def send(k, c):
+        d, copy = part_of(k, c)
+        pl.when(exists(d))(lambda: copy.start())
+
+
+    def sum_chunk(c, _):
+        base = c * planes
+        part = pl.ds(base, planes)
+        pltpu.make_async_copy(w_hbm.at[part], wb.at[part], img_sem.at[0, c]).wait()
+        pltpu.make_async_copy(f_hbm.at[part], fb.at[part], img_sem.at[1, c]).wait()
+        h = c // 2
+        group = lane64 // 4 - 16 * (c % 2)
+        packed = hzs[h]
+        for j in range(planes):
+            w = wb[base + j]
+            f = fb[base + j]
+            s = w + f
+            diff[base + j] = w - f
+            sp[base + j + 2, 8:72, :] = s
+            hys[0, base + j] = s[0:2]
+            hys[1, base + j] = s[62:64]
+            turned = roll(s, 64 * (c % 2) + 4 * j + 2, 1)
+            packed = jnp.where(group == j, turned, packed)
+        hzs[h] = packed
+        return 0
+
+    for c in range(chunks):
+        sum_chunk(c, 0)
+        if c == 1:
+            pl.semaphore_wait(bar, count)
+            for k in (2, 3):
+                send(k, 0)
+            send(0, 0)
+        if c > 0:
+            for k in (2, 3):
+                send(k, c)
+        if c % 2:
+            for k in (4, 5):
+                send(k, c)
+    send(1, 0)
 
     small[0].wait()
 
@@ -258,7 +286,7 @@
                 dzb[base + 8 * half + j] = out[64 * j : 64 * (j + 1)]
         return 0
 
-    lax.fori_loop(0, 4, dz_chunk, 0)
+    lax.fori_loop(0, 4, dz_chunk, 0, unroll=True)
 
     small[1].wait()
 
@@ -325,7 +353,7 @@
 
 
 def gradient(dims, sp, diff, dzb, cz, e0, cctl_h, wy_h, wz_h, h_h, fine_out, coarse_out,
-             cctl, wy, wz, h_w, small_sem, dz2, xs, zs, e, csend, crecv, yg, xg, mix,
+             cctl, wy, wz, h_w, small_sem, dz2, xs, zs, e, csend, crecv, xg, total_rows, mix,
              fxr, fys, fyr, fzs, fzr, cs, cr, gs, gr, fs, fr):
     nx, ny, nz = dims
     here = Place(dims)
@@ -344,23 +372,21 @@
         copy.start()
 
     bar = pltpu.get_barrier_semaphore()
+    plane = sorted(((ox, oy) for ox in range(nx) for oy in range(ny) if ox or oy),
+                   key=lambda o: -min(o[1], ny - o[1]) - 0.5 * min(o[0], nx - o[0]))
+
+    def in_plane(ox, oy):
+        return (lax.rem(gx + ox, nx), lax.rem(gy + oy, ny), gz)
+
     for dx, dy in sides:
         def greet(dx=dx, dy=dy):
-            for o in ring_order(nz):
-                if dx or dy or o:
-                    pl.semaphore_signal(bar, inc=1, device_id=beside(dx, dy, o), device_id_type=MESH)
+            for o in ring_order(nz)[:-1]:
+                pl.semaphore_signal(bar, inc=1, device_id=beside(dx, dy, o), device_id_type=MESH)
         if_seen(dx, dy, greet)
-    for axis in range(2):
-        for o in range(2, dims[axis] - 1):
-            device, t = ring(axis, o)
-            pl.when(jnp.abs(t - pos[axis]) > 1)(lambda device=device: pl.semaphore_signal(
-                bar, inc=1, device_id=device, device_id_type=MESH))
-        for o in (1, dims[axis] - 1):
-            device, t = ring(axis, o)
-            pl.when(jnp.abs(t - pos[axis]) > 1)(lambda device=device: pl.semaphore_signal(
-                bar, inc=1, device_id=device, device_id_type=MESH))
+    for ox, oy in plane:
+        pl.semaphore_signal(bar, inc=1, device_id=in_plane(ox, oy), device_id_type=MESH)
     wide = [1 + h[-1].astype(jnp.int32) + h[1].astype(jnp.int32) for h in has]
-    greeted = wide[0] * wide[1] * nz - 1 + (nx - wide[0]) + (ny - wide[1])
+    greeted = wide[0] * wide[1] * (nz - 1) + nx * ny - 1
 
     for side, d in ((0, -1), (1, 1)):
         for axis, ref in enumerate((fxr, fyr, fzr)):
@@ -400,7 +426,7 @@
                 dz2[base + 8 * half + j] = dzb[base + 8 * half + j] + out[64 * j : 64 * (j + 1)]
         return 0
 
-    lax.fori_loop(0, 4, z_fix, 0)
+    lax.fori_loop(0, 4, z_fix, 0, unroll=True)
 
     groups = 16
     slabs = groups + 3
@@ -482,14 +508,14 @@
         slot = 3 * (dx + 1) + dy + 1
         return pltpu.make_async_remote_copy(
             src_ref=csend.at[dx + 1, pl.ds(2 * (dy + 1), 1), :], dst_ref=crecv.at[slot, pl.ds(gz, 1), :],
-            send_sem=cs.at[slot, o], recv_sem=cr.at[slot, o], device_id=beside(dx, dy, o), device_id_type=MESH)
-
-    def coarse_arrival(dx, dy, o):
+            send_sem=cs.at[slot], recv_sem=cr.at[slot], device_id=beside(dx, dy, o), device_id_type=MESH)
+
+    def coarse_line(dx, dy):
         slot = 3 * (dx + 1) + dy + 1
-        s = lax.rem(gz + nz - o, nz)
+        rows = crecv.at[slot] if dx or dy else crecv.at[slot, pl.ds(0, nz - 1), :]
         return pltpu.make_async_remote_copy(
-            src_ref=csend.at[dx + 1, pl.ds(2 * (dy + 1), 1), :], dst_ref=crecv.at[slot, pl.ds(s, 1), :],
-            send_sem=cs.at[slot, o], recv_sem=cr.at[slot, o], device_id=beside(dx, dy, o), device_id_type=MESH)
+            src_ref=rows, dst_ref=rows, send_sem=cs.at[slot], recv_sem=cr.at[slot],
+            device_id=beside(0, 0, 1), device_id_type=MESH)
 
     def coarse_all(fn):
         for o in ring_order(nz):
@@ -510,45 +536,6 @@
             e[a, j] = v
     for k in (0, 1):
         start(fine_copy, k)
-
-    coarse_all(lambda dx, dy, o: if_seen(-dx, -dy, lambda: coarse_arrival(dx, dy, o).wait_recv()))
-    line = crecv[0]
-    for i in range(1, 9):
-        line = line + crecv[i]
-    line = pltpu.roll(line, 0, 1, stride=4, stride_axis=0)
-    place = lane8 % 32 + 2 - 4 * lax.broadcasted_iota(jnp.int32, (8, 128), 0)
-    for a in range(3):
-        piece = jnp.where((place >= 0) & (place < 8), roll(line, -2 - 8 * a, 1), 0.0)
-        yg[a, pl.ds(gy, 1), :] = jnp.sum(piece, axis=0, keepdims=True)
-
-    def gather_copy(axis, o):
-        device, _ = ring(axis, o)
-        if axis == 1:
-            src = dst = yg.at[:, pl.ds(gy, 1), :]
-        else:
-            src, dst = yg, xg.at[gx]
-        return pltpu.make_async_remote_copy(
-            src_ref=src, dst_ref=dst, send_sem=gs.at[axis, o], recv_sem=gr.at[axis, o],
-            device_id=device, device_id_type=MESH)
-
-    def offsets(axis):
-        return ring_order(dims[axis])[:-1]
-
-    def gather_start(axis):
-        for o in offsets(axis):
-            gather_copy(axis, o).start()
-
-    def gather_wait(axis):
-        n = dims[axis]
-        for o in reversed(offsets(axis)):
-            s = lax.rem(pos[axis] + n - o, n)
-            dst = (xg.at[s], yg.at[:, pl.ds(s, 1), :])[axis]
-            src = yg if axis == 0 else dst
-            pltpu.make_async_remote_copy(
-                src_ref=src, dst_ref=dst, send_sem=gs.at[axis, o], recv_sem=gr.at[axis, o],
-                device_id=ring(axis, o)[0], device_id_type=MESH).wait_recv()
-
-    gather_start(1)
 
     kx, ky, kz = cctl.shape[1:]
     shape = (ky, kz)
@@ -591,9 +578,30 @@
     for k in (2, 3):
         start(fine_copy, k)
 
-    gather_wait(1)
-    xg[gx] = yg[...]
-    gather_start(0)
+    for dx, dy in sides:
+        if_seen(-dx, -dy, lambda: coarse_line(dx, dy).wait_recv())
+    line = crecv[0]
+    for i in range(1, 9):
+        line = line + crecv[i]
+    line = pltpu.roll(line, 0, 1, stride=4, stride_axis=0)
+    place = lane8 % 32 + 2 - 4 * lax.broadcasted_iota(jnp.int32, (8, 128), 0)
+    for a in range(3):
+        piece = jnp.where((place >= 0) & (place < 8), roll(line, -2 - 8 * a, 1), 0.0)
+        xg[gx, a, pl.ds(gy, 1), :] = jnp.sum(piece, axis=0, keepdims=True)
+
+    def gather_copy(ox, oy, sx, sy):
+        slot = xg.at[sx, :, pl.ds(sy, 1), :]
+        return pltpu.make_async_remote_copy(
+            src_ref=slot, dst_ref=slot, send_sem=gs, recv_sem=gr,
+            device_id=in_plane(ox, oy), device_id_type=MESH)
+
+    def gather_plane():
+        return pltpu.make_async_remote_copy(
+            src_ref=total_rows, dst_ref=total_rows, send_sem=gs, recv_sem=gr,
+            device_id=in_plane(0, 1), device_id_type=MESH)
+
+    for ox, oy in plane:
+        gather_copy(ox, oy, gx, gy).start()
 
     for k in (2, 3):
         arrived(fine_copy, k)
@@ -627,7 +635,7 @@
             v = v + jnp.where((lane8 >= 14) & (lane8 < 16), roll(p1, 14 - 2 * s, 1), 0.0)
             fine_out[a, j] = v[:, :16]
 
-    gather_wait(0)
+    gather_plane().wait_recv()
     for g in range(nx):
         for a in range(3):
             rows = xg[g, a]
@@ -640,17 +648,15 @@
 
     for k in range(2, 6):
         sent(fine_copy, k)
-    coarse_all(lambda dx, dy, o: if_seen(dx, dy, lambda: coarse_copy(dx, dy, o).wait_send()))
-    for axis in range(2):
-        for o in range(1, dims[axis]):
-            gather_copy(axis, o).wait_send()
+    for dx, dy in sides:
+        if_seen(dx, dy, lambda: coarse_line(dx, dy).wait_send())
+    gather_plane().wait_send()
 
 
 def per_device(dims, warped_image, fixed_image, fine_control, coarse_control):
     sx, sy, sz = warped_image.shape
     kx, ky, kz = coarse_control.shape[1:]
     nx, ny, nz = dims
-    wide = max(dims)
     slabs = 19
     vmem = pl.BlockSpec(memory_space=pltpu.VMEM)
     hbm = pl.BlockSpec(memory_space=pltpu.HBM)
@@ -667,7 +673,7 @@
         scratch_shapes=[
             v(*fine_control.shape), h(2 * sz, sz), dma((2,)), v(sx, sy, sz), v(sx, sy, sz),
             v(2, sx, 2, sz), v(2, sx, 2, sz), v(2, sy, 128), v(2, 2, sy, 128), v(12, 16, 128),
-            dma((2, 8)), dma((6,)), dma((6,)),
+            dma((2, 4)), dma((6,)), dma((6,)),
         ],
         compiler_params=pltpu.CompilerParams(collective_id=0, has_side_effects=True, vmem_limit_bytes=24 << 20),
         name="layers",
@@ -680,9 +686,9 @@
         scratch_shapes=[
             v(*coarse_control.shape), h(48, 2 * sy), h(4, 2 * sz, 256), h(256, sz), dma((4,)),
             v(sx, sy, sz), v(sy, 3 * slabs * 128), v(3, slabs, 16, 128), v(3, 12, 16, 128),
-            v(3, 8, 128), v(9, nz, 128), v(3, ny, 128), v(nx, 3, ny, 128), v(3, kx, ky, 128),
+            v(3, 8, 128), v(9, nz, 128), v(nx, 3, ny, 128), v(3 * (nx * ny - 1), 128), v(3, kx, ky, 128),
             v(2, 3, 2, 16, 128), v(2, 24, 2, 128), v(2, 24, 2, 128), v(2, 8, 128), v(2, 8, 128),
-            dma((9, nz)), dma((9, nz)), dma((2, wide)), dma((2, wide)), dma((6,)), dma((6,)),
+            dma((9,)), dma((9,)), dma, dma, dma((6,)), dma((6,)),
         ],
         compiler_params=pltpu.CompilerParams(collective_id=1, has_side_effects=True, vmem_limit_bytes=24 << 20),
         name="gradient",

time: 43.7 us -> 39.1 us (0.89)
  Pallas kernels: 41.4 us -> 36.9 us
    pallas_call x1, Pallas kernels: 30.2 us -> 25.7 us  [per_device(): pl.pallas_call(lambda *refs: gradient(dims, *refs), out_shape=(out(*fine_...]
where the time goes in v2:
time: 39.1 us; the launch traced here: 38.9 us
  Pallas kernels  36.9 us (94%)
  local copies, waits for them, and re-layouts  1.39 us (4%)
  between operations  0.65 us (2%)
    pallas_call x1, Pallas kernels, per_device(): pl.pallas_call(lambda *refs: gradient(dims, *refs), out_shape=(out(*fine_...  25.7 us
    pallas_call x1, Pallas kernels, per_device(): pl.pallas_call(lambda *refs: layers(dims, *refs), out_shape=(out(sx + 4,...  11.2 us
    unnamed x2, local copies, waits for them, and re-layouts  1.39 us

profile of v2, /device:TPU:1, one launch (start us, length us, event | category | flops | bytes accessed | tf_op | source)
XLA Modules:
  0.0 38.9 jit_solution(12113474145065080785)
XLA Ops:
  0.6 11.2 %layers.1 = (f32[68,80,128]{2,1,0:T(8,128)S(1)}, f32[64,64,128]{2,1,0:T(8,128)S(1)}, f32[64,64,128]{2,1,0:T(8,128)S(1)}, f32[2,64,128]{2,1,0:T(8,128)S(1)}, f32[3,12,16,128]{3,2,1,0:T(8,128)S(1)}) custom-call(f32[64,64,128]{2,1,0:T(8,128)} %refs_0_.1, f32[64,64,128]{2,1,0:T(8,128)} %refs_1_.1, f32[3,8,8,16]{3,2,1,0:T(8,128)} %refs_2_.1, ...), custom_call_target="tpu_custom_call" | custom-call | tf_op jit(solution)/shard_map/layers/pallas_call | solution.py:668
  11.8 25.7 %gradient.1 = (f32[3,8,8,16]{3,2,1,0:T(8,128)S(1)}, f32[3,16,16,32]{3,2,1,0:T(8,128)S(1)}) custom-call(f32[68,80,128]{2,1,0:T(8,128)S(1)} %get-tuple-element.7.refs_0_, f32[64,64,128]{2,1,0:T(8,128)S(1)} %get-tuple-element.8.refs_1_, f32[64,64,128]{2,1,0:T(8,128)S(1)} %get-tuple-element.9.refs_2_, f32[2,64,128]{2,1,0:T(8,128)S(1)} %get-tuple-element.10.refs_3_, ...), custom_call_target="tpu_custom_call" | custom-call | tf_op jit(solution)/shard_map/gradient/pallas_call | solution.py:681
  37.5 0.6 %copy.12 = f32[3,8,8,16]{3,2,1,0:T(8,128)} copy(f32[3,8,8,16]{3,2,1,0:T(8,128)S(1)} %get-tuple-element.14) | data formatting | bytes 24576
  38.2 0.7 %copy.13 = f32[3,16,16,32]{3,2,1,0:T(8,128)} copy(f32[3,16,16,32]{3,2,1,0:T(8,128)S(1)} %get-tuple-element.15) | data formatting | bytes 196608

commit v3 on v2

--- a/solution.py
+++ b/solution.py
@@ -158,8 +158,10 @@
 SIDES = list(itertools.product((-1, 0, 1), repeat=2))
 
 
-def layers(dims, w_hbm, f_hbm, ctl_h, dz_h, sp, diff, dzb, cz, e,
-           ctl, dz_w, small_sem, wb, fb, hys, hyr, hzs, hzr, fw, img_sem, hs, hr):
+def gradient(dims, w_hbm, f_hbm, ctl_h, cctl_h, dz_h, h_h, wy_h, wz_h, fine_out, coarse_out,
+             ctl, cctl, dz_w, h_w, wy, wz, small_sem, wb, fb, sp, diff, dzb, cz, e,
+             hys, hyr, hzs, hzr, fw, xs, zs, csend, crecv, xg, total_rows, mix,
+             fxr, fys, fyr, fzs, fzr, img_sem, hs, hr, cs, cr, gs, gr, fs, fr, near_sem, far_sem):
     nx, ny, nz = dims
     here = Place(dims)
     pos = here.pos
@@ -172,12 +174,71 @@
     lane64 = lanes((64, 128))
 
     bar = pltpu.get_barrier_semaphore()
-    count = 0
-    for axis in range(3):
-        for side in (-1, 1):
-            d = tuple(side if i == axis else 0 for i in range(3))
-            pl.when(exists(d))(lambda d=d: pl.semaphore_signal(bar, inc=1, device_id=at(d), device_id_type=MESH))
-            count = count + has[axis][side].astype(jnp.int32)
+    odd = lax.rem(gx + gy + gz, 2) == 1
+    even = jnp.logical_not(odd)
+    faces = [tuple(side if i == axis else 0 for i in range(3)) for axis in range(3) for side in (-1, 1)]
+    count = sum(has[axis][side].astype(jnp.int32) for axis in range(3) for side in (-1, 1))
+
+    def greet_faces(sem):
+        for d in faces:
+            pl.when(exists(d))(lambda: pl.semaphore_signal(sem, inc=1, device_id=at(d), device_id_type=MESH))
+
+    @pl.when(even)
+    def _():
+        greet_faces(bar)
+
+    def near_done():
+        @pl.when(odd)
+        def _():
+            pl.semaphore_wait(bar, count)
+            greet_faces(near_sem)
+
+        @pl.when(even)
+        def _():
+            pl.semaphore_wait(near_sem, count)
+
+    chip = gx // 2
+    lean = 2 * lax.rem(gx, 2) - 1
+    next_chip = chip + lean
+    has_next = (next_chip >= 0) & (next_chip < nx // 2)
+    partner = (gx - lean, gy, gz)
+
+    def greet_chip(c, y, z):
+        device = (2 * c + lax.rem(y + z, 2), y, z)
+        pl.semaphore_signal(bar, inc=1, device_id=device, device_id_type=MESH)
+
+    def far_greetings():
+        for dy in (-1, 1, 0):
+            def line(dy=dy):
+                for o in ring_order(nz)[:-1]:
+                    greet_chip(chip, gy + dy, lax.rem(gz + o, nz))
+
+                @pl.when(has_next)
+                def _():
+                    for o in ring_order(nz)[:-1]:
+                        greet_chip(next_chip, gy + dy, lax.rem(gz + o, nz))
+            if_seen(0, dy, line)
+        for oc in range(nx // 2):
+            for oy in ring_order(ny):
+                def one(oc=oc, oy=oy):
+                    greet_chip(lax.rem(chip + oc, nx // 2), lax.rem(gy + oy, ny), gz)
+                if oc or oy:
+                    one()
+                else:
+                    pl.when(odd)(one)
+
+    def far_done():
+        wide_x = 4 - (chip == 0).astype(jnp.int32) - (chip == nx // 2 - 1).astype(jnp.int32)
+        wide_y = 1 + has[1][-1].astype(jnp.int32) + has[1][1].astype(jnp.int32)
+
+        @pl.when(even)
+        def _():
+            pl.semaphore_wait(bar, wide_x * wide_y * (nz - 1) + nx * ny - 1)
+            pl.semaphore_signal(far_sem, inc=1, device_id=partner, device_id_type=MESH)
+
+        @pl.when(odd)
+        def _():
+            pl.semaphore_wait(far_sem, 1)
 
     chunks = 4
     planes = 16
@@ -185,9 +246,11 @@
         part = pl.ds(c * planes, planes)
         pltpu.make_async_copy(w_hbm.at[part], wb.at[part], img_sem.at[0, c]).start()
         pltpu.make_async_copy(f_hbm.at[part], fb.at[part], img_sem.at[1, c]).start()
-    small = [pltpu.make_async_copy(dz_h, dz_w, small_sem.at[0]), pltpu.make_async_copy(ctl_h, ctl, small_sem.at[1])]
+    small = [pltpu.make_async_copy(src, dst, small_sem.at[i]) for i, (src, dst) in enumerate(
+        ((dz_h, dz_w), (ctl_h, ctl), (h_h, h_w), (wy_h, wy), (wz_h, wz), (cctl_h, cctl)))]
     for copy in small:
         copy.start()
+    far_greetings()
 
     for side, d in ((0, -1), (1, 1)):
         @pl.when(jnp.logical_not(has[0][d]))
@@ -263,7 +326,7 @@
     for c in range(chunks):
         sum_chunk(c, 0)
         if c == 1:
-            pl.semaphore_wait(bar, count)
+            near_done()
             for k in (2, 3):
                 send(k, 0)
             send(0, 0)
@@ -287,6 +350,17 @@
         return 0
 
     lax.fori_loop(0, 4, dz_chunk, 0, unroll=True)
+
+    for side, d in ((0, -1), (1, 1)):
+        for axis, ref in enumerate((fxr, fyr, fzr)):
+            @pl.when(jnp.logical_not(has[axis][d]))
+            def _(side=side, ref=ref):
+                ref[side] = jnp.zeros(ref.shape[1:], F32)
+    for dx, dy in sides:
+        if dx or dy:
+            @pl.when(jnp.logical_not(seen(-dx, -dy)))
+            def _(dx=dx, dy=dy):
+                crecv[3 * (dx + 1) + dy + 1] = zero8
 
     small[1].wait()
 
@@ -348,56 +422,11 @@
         a_part = jnp.where(m4 < 2, -roll(u, -2, 1), roll(u, 2, 1))
         b_part = jnp.where(m4 == 1, 8.0 * roll(u, -1, 1), jnp.where(m4 == 2, -8.0 * roll(u, 1, 1), 0.0))
         cz[h] = a_part + b_part
-    for k in range(6):
-        sent(halo, k)
-
-
-def gradient(dims, sp, diff, dzb, cz, e0, cctl_h, wy_h, wz_h, h_h, fine_out, coarse_out,
-             cctl, wy, wz, h_w, small_sem, dz2, xs, zs, e, csend, crecv, xg, total_rows, mix,
-             fxr, fys, fyr, fzs, fzr, cs, cr, gs, gr, fs, fr):
-    nx, ny, nz = dims
-    here = Place(dims)
-    pos = here.pos
-    gx, gy, gz = pos
-    has, exists, at, ring, seen, if_seen, beside = (
-        here.has, here.exists, here.at, here.ring, here.seen, here.if_seen, here.beside)
-    start, sent, arrived = here.start, here.sent, here.arrived
-    sides = SIDES
-    zero8 = jnp.zeros((8, 128), F32)
-    lane64 = lanes((64, 128))
-
-    small = [pltpu.make_async_copy(src, dst, small_sem.at[i]) for i, (src, dst) in enumerate(
-        ((h_h, h_w), (wy_h, wy), (wz_h, wz), (cctl_h, cctl)))]
-    for copy in small:
-        copy.start()
-
-    bar = pltpu.get_barrier_semaphore()
     plane = sorted(((ox, oy) for ox in range(nx) for oy in range(ny) if ox or oy),
                    key=lambda o: -min(o[1], ny - o[1]) - 0.5 * min(o[0], nx - o[0]))
 
     def in_plane(ox, oy):
         return (lax.rem(gx + ox, nx), lax.rem(gy + oy, ny), gz)
-
-    for dx, dy in sides:
-        def greet(dx=dx, dy=dy):
-            for o in ring_order(nz)[:-1]:
-                pl.semaphore_signal(bar, inc=1, device_id=beside(dx, dy, o), device_id_type=MESH)
-        if_seen(dx, dy, greet)
-    for ox, oy in plane:
-        pl.semaphore_signal(bar, inc=1, device_id=in_plane(ox, oy), device_id_type=MESH)
-    wide = [1 + h[-1].astype(jnp.int32) + h[1].astype(jnp.int32) for h in has]
-    greeted = wide[0] * wide[1] * (nz - 1) + nx * ny - 1
-
-    for side, d in ((0, -1), (1, 1)):
-        for axis, ref in enumerate((fxr, fyr, fzr)):
-            @pl.when(jnp.logical_not(has[axis][d]))
-            def _(side=side, ref=ref):
-                ref[side] = jnp.zeros(ref.shape[1:], F32)
-    for dx, dy in sides:
-        if dx or dy:
-            @pl.when(jnp.logical_not(seen(-dx, -dy)))
-            def _(dx=dx, dy=dy):
-                crecv[3 * (dx + 1) + dy + 1] = zero8
 
     def fine_copy(k):
         axis, side = k // 2, k % 2
@@ -413,7 +442,7 @@
             src_ref=src, dst_ref=dst, send_sem=fs.at[k], recv_sem=fr.at[k],
             device_id=at(d), device_id_type=MESH)
 
-    small[0].wait()
+    small[2].wait()
 
     def z_fix(c, _):
         base = pl.multiple_of(c * 16, 16)
@@ -423,7 +452,7 @@
             parts = [jnp.concatenate(split(jnp.where(group == j, layer, 0.0)), 1) for j in range(8)]
             out = jnp.dot(jnp.concatenate(parts, 0), h_w[...], preferred_element_type=F32)
             for j in range(8):
-                dz2[base + 8 * half + j] = dzb[base + 8 * half + j] + out[64 * j : 64 * (j + 1)]
+                dzb[base + 8 * half + j] = dzb[base + 8 * half + j] + out[64 * j : 64 * (j + 1)]
         return 0
 
     lax.fori_loop(0, 4, z_fix, 0, unroll=True)
@@ -451,7 +480,7 @@
                     yp1 = sp[plane, pl.ds(r0 + 9, 8), :]
                     yp2 = sp[plane, pl.ds(r0 + 10, 8), :]
                     sy = (ym2 - yp2) + 8.0 * (yp1 - ym1)
-                    sz = dz2[x0 + i, pl.ds(r0, 8), :]
+                    sz = dzb[x0 + i, pl.ds(r0, 8), :]
                     dv = diff[x0 + i, pl.ds(r0, 8), :]
                     for a, s in enumerate((sx, sy, sz)):
                         f = dv * s
@@ -470,7 +499,7 @@
 
     lax.fori_loop(0, 8, column, 0)
 
-    for copy in small[1:]:
+    for copy in small[3:]:
         copy.wait()
     total = None
     for a in range(3):
@@ -523,12 +552,12 @@
                 if o or dx or dy:
                     fn(dx, dy, o)
 
-    pl.semaphore_wait(bar, greeted)
+    far_done()
     coarse_all(lambda dx, dy, o: if_seen(dx, dy, lambda: coarse_copy(dx, dy, o).start()))
 
     for a in range(3):
         for j in range(12):
-            v = e0[a, j]
+            v = e[a, j]
             for k in range(5):
                 i = 2 * j - 4 + k
                 if 0 <= i < slabs:
@@ -646,6 +675,8 @@
         for j in range(kx):
             coarse_out[a, j] = coarse_out[a, j] + mix[a, j][:, :kz]
 
+    for k in range(6):
+        sent(halo, k)
     for k in range(2, 6):
         sent(fine_copy, k)
     for dx, dy in sides:
@@ -664,35 +695,27 @@
     h = lambda *shape: pltpu.VMEM(shape, BF16)
     out = lambda *shape: jax.ShapeDtypeStruct(shape, F32)
     dma = pltpu.SemaphoreType.DMA
+    flag = pltpu.SemaphoreType.REGULAR
     far = lambda x: pltpu.with_memory_space_constraint(jnp.asarray(x), pltpu.HBM)
-    local = pl.pallas_call(
-        lambda *refs: layers(dims, *refs),
-        out_shape=(out(sx + 4, sy + 16, sz), out(sx, sy, sz), out(sx, sy, sz), out(2, sy, 128), out(3, 12, 16, 128)),
-        in_specs=[hbm] * 4,
-        out_specs=(vmem,) * 5,
-        scratch_shapes=[
-            v(*fine_control.shape), h(2 * sz, sz), dma((2,)), v(sx, sy, sz), v(sx, sy, sz),
-            v(2, sx, 2, sz), v(2, sx, 2, sz), v(2, sy, 128), v(2, 2, sy, 128), v(12, 16, 128),
-            dma((2, 4)), dma((6,)), dma((6,)),
-        ],
-        compiler_params=pltpu.CompilerParams(collective_id=0, has_side_effects=True, vmem_limit_bytes=24 << 20),
-        name="layers",
-    )(far(warped_image), far(fixed_image), far(fine_control), far(d_matrix(sz)))
     return pl.pallas_call(
         lambda *refs: gradient(dims, *refs),
         out_shape=(out(*fine_control.shape), out(*coarse_control.shape)),
-        in_specs=[vmem] * 5 + [hbm] * 4,
+        in_specs=[hbm] * 8,
         out_specs=(vmem, vmem),
         scratch_shapes=[
-            v(*coarse_control.shape), h(48, 2 * sy), h(4, 2 * sz, 256), h(256, sz), dma((4,)),
-            v(sx, sy, sz), v(sy, 3 * slabs * 128), v(3, slabs, 16, 128), v(3, 12, 16, 128),
-            v(3, 8, 128), v(9, nz, 128), v(nx, 3, ny, 128), v(3 * (nx * ny - 1), 128), v(3, kx, ky, 128),
+            v(*fine_control.shape), v(*coarse_control.shape), h(2 * sz, sz), h(256, sz), h(48, 2 * sy),
+            h(4, 2 * sz, 256), dma((6,)), v(sx, sy, sz), v(sx, sy, sz), v(sx + 4, sy + 16, sz), v(sx, sy, sz),
+            v(sx, sy, sz), v(2, sy, 128), v(3, 12, 16, 128),
+            v(2, sx, 2, sz), v(2, sx, 2, sz), v(2, sy, 128), v(2, 2, sy, 128), v(12, 16, 128),
+            v(sy, 3 * slabs * 128), v(3, slabs, 16, 128), v(3, 8, 128), v(9, nz, 128),
+            v(nx, 3, ny, 128), v(3 * (nx * ny - 1), 128), v(3, kx, ky, 128),
             v(2, 3, 2, 16, 128), v(2, 24, 2, 128), v(2, 24, 2, 128), v(2, 8, 128), v(2, 8, 128),
-            dma((9,)), dma((9,)), dma, dma, dma((6,)), dma((6,)),
+            dma((2, 4)), dma((6,)), dma((6,)), dma((9,)), dma((9,)), dma, dma, dma((6,)), dma((6,)), flag, flag,
         ],
-        compiler_params=pltpu.CompilerParams(collective_id=1, has_side_effects=True, vmem_limit_bytes=24 << 20),
+        compiler_params=pltpu.CompilerParams(collective_id=0, has_side_effects=True, vmem_limit_bytes=48 << 20),
         name="gradient",
-    )(*local, far(coarse_control), far(y_matrix(sy)), far(z_matrices(sz)), far(h_matrix(sz)))
+    )(far(warped_image), far(fixed_image), far(fine_control), far(coarse_control), far(d_matrix(sz)),
+      far(h_matrix(sz)), far(y_matrix(sy)), far(z_matrices(sz)))
 
 
 def solution(mesh):

time: 39.1 us -> 38.4 us (0.982)
  Pallas kernels: 36.9 us -> 36.3 us
    pallas_call x1 -> x0, Pallas kernels: 11.2 us -> none  [per_device(): pl.pallas_call(lambda *refs: layers(dims, *refs), out_shape=(out(sx + 4,...]
    pallas_call x1, Pallas kernels: 25.7 us -> 36.3 us  [per_device(): pl.pallas_call(lambda *refs: gradient(dims, *refs), out_shape=(out(*fine_...]
where the time goes in v3:
time: 38.4 us; the launch traced here: 38.3 us
  Pallas kernels  36.3 us (95%)
  local copies, waits for them, and re-layouts  1.39 us (4%)
  between operations  0.64 us (2%)
    pallas_call x1, Pallas kernels, per_device(): pl.pallas_call(lambda *refs: gradient(dims, *refs), out_shape=(out(*fine_...  36.3 us
    unnamed x2, local copies, waits for them, and re-layouts  1.39 us

profile of v3, /device:TPU:1, one launch (start us, length us, event | category | flops | bytes accessed | tf_op | source)
XLA Modules:
  0.0 38.3 jit_solution(1034889566930658)
XLA Ops:
  0.6 36.3 %gradient.1 = (f32[3,8,8,16]{3,2,1,0:T(8,128)S(1)}, f32[3,16,16,32]{3,2,1,0:T(8,128)S(1)}) custom-call(f32[64,64,128]{2,1,0:T(8,128)} %refs_0_.1, f32[64,64,128]{2,1,0:T(8,128)} %refs_1_.1, f32[3,8,8,16]{3,2,1,0:T(8,128)} %refs_2_.1, f32[3,16,16,32]{3,2,1,0:T(8,128)} %refs_3_.1, bf16[256,128]{1,0:T(8,128)(2,1)} %constant.8.clone.refs_4_, ...), custom_call_target="tpu_custom_call" | custom-call | tf_op jit(solution)/shard_map/gradient/pallas_call | solution.py:700
  36.9 0.6 %copy.12 = f32[3,8,8,16]{3,2,1,0:T(8,128)} copy(f32[3,8,8,16]{3,2,1,0:T(8,128)S(1)} %get-tuple-element.4) | data formatting | bytes 24576
  37.5 0.7 %copy.13 = f32[3,16,16,32]{3,2,1,0:T(8,128)} copy(f32[3,16,16,32]{3,2,1,0:T(8,128)S(1)} %get-tuple-element.5) | data formatting | bytes 196608

commit v4 on v3

--- a/solution.py
+++ b/solution.py
@@ -160,7 +160,7 @@
 
 def gradient(dims, w_hbm, f_hbm, ctl_h, cctl_h, dz_h, h_h, wy_h, wz_h, fine_out, coarse_out,
              ctl, cctl, dz_w, h_w, wy, wz, small_sem, wb, fb, sp, diff, dzb, cz, e,
-             hys, hyr, hzs, hzr, fw, xs, zs, csend, crecv, xg, total_rows, mix,
+             hxr, hys, hyr, hzs, hzr, fw, xs, zs, csend, crecv, xg, total_rows, mix,
              fxr, fys, fyr, fzs, fzr, img_sem, hs, hr, cs, cr, gs, gr, fs, fr, near_sem, far_sem):
     nx, ny, nz = dims
     here = Place(dims)
@@ -203,25 +203,31 @@
     has_next = (next_chip >= 0) & (next_chip < nx // 2)
     partner = (gx - lean, gy, gz)
 
-    def greet_chip(c, y, z):
-        device = (2 * c + lax.rem(y + z, 2), y, z)
+    same = lax.rem(gy + gz, 2)
+    parity = (same, 1 - same)
+    line_z = [lax.rem(gz + o, nz) for o in range(nz)]
+    line_y = [lax.rem(gy + o, ny) for o in range(ny)]
+
+    def greet_chip(first, y, z, steps):
+        device = (first + parity[steps % 2], y, z)
         pl.semaphore_signal(bar, inc=1, device_id=device, device_id_type=MESH)
 
     def far_greetings():
         for dy in (-1, 1, 0):
             def line(dy=dy):
                 for o in ring_order(nz)[:-1]:
-                    greet_chip(chip, gy + dy, lax.rem(gz + o, nz))
+                    greet_chip(2 * chip, gy + dy, line_z[o], dy + o)
 
                 @pl.when(has_next)
                 def _():
                     for o in ring_order(nz)[:-1]:
-                        greet_chip(next_chip, gy + dy, lax.rem(gz + o, nz))
+                        greet_chip(2 * next_chip, gy + dy, line_z[o], dy + o)
             if_seen(0, dy, line)
         for oc in range(nx // 2):
+            first = 2 * lax.rem(chip + oc, nx // 2)
             for oy in ring_order(ny):
-                def one(oc=oc, oy=oy):
-                    greet_chip(lax.rem(chip + oc, nx // 2), lax.rem(gy + oy, ny), gz)
+                def one(first=first, oy=oy):
+                    greet_chip(first, line_y[oy], gz, oy)
                 if oc or oy:
                     one()
                 else:
@@ -240,8 +246,8 @@
         def _():
             pl.semaphore_wait(far_sem, 1)
 
-    chunks = 4
-    planes = 16
+    chunks = 8
+    planes = 8
     for c in range(chunks):
         part = pl.ds(c * planes, planes)
         pltpu.make_async_copy(w_hbm.at[part], wb.at[part], img_sem.at[0, c]).start()
@@ -255,7 +261,7 @@
     for side, d in ((0, -1), (1, 1)):
         @pl.when(jnp.logical_not(has[0][d]))
         def _(side=side):
-            sp[66 * side : 66 * side + 2, 8:72, :] = jnp.zeros((2, 64, 128), F32)
+            hxr[side] = jnp.zeros(hxr.shape[1:], F32)
 
         @pl.when(jnp.logical_not(has[1][d]))
         def _(side=side):
@@ -266,6 +272,8 @@
             hzr[side] = jnp.zeros(hzr.shape[1:], F32)
 
     hzs[...] = jnp.zeros(hzs.shape, F32)
+    for first in (0, 66):
+        sp[first : first + 2, 8:72, :] = jnp.zeros((2, 64, 128), F32)
 
     def halo(k):
         axis, side = k // 2, k % 2
@@ -273,7 +281,7 @@
         d[axis] = 2 * side - 1
         if axis == 0:
             src = sp.at[pl.ds(2 if side == 0 else 64, 2), pl.ds(8, 64), :]
-            dst = sp.at[pl.ds(66 if side == 0 else 0, 2), pl.ds(8, 64), :]
+            dst = hxr.at[1 - side]
         elif axis == 1:
             src, dst = hys.at[side], hyr.at[1 - side]
         else:
@@ -292,7 +300,7 @@
             part = pl.ds(c * planes, planes)
             src, dst = hys.at[side, part], hyr.at[1 - side, part]
         else:
-            src, dst = hzs.at[c // 2], hzr.at[1 - side, c // 2]
+            src, dst = hzs.at[c // 4], hzr.at[1 - side, c // 4]
         return d, pltpu.make_async_remote_copy(
             src_ref=src, dst_ref=dst, send_sem=hs.at[k], recv_sem=hr.at[k],
             device_id=at(d), device_id_type=MESH)
@@ -307,8 +315,8 @@
         part = pl.ds(base, planes)
         pltpu.make_async_copy(w_hbm.at[part], wb.at[part], img_sem.at[0, c]).wait()
         pltpu.make_async_copy(f_hbm.at[part], fb.at[part], img_sem.at[1, c]).wait()
-        h = c // 2
-        group = lane64 // 4 - 16 * (c % 2)
+        h = c // 4
+        group = lane64 // 4 - 8 * (c % 4)
         packed = hzs[h]
         for j in range(planes):
             w = wb[base + j]
@@ -318,26 +326,26 @@
             sp[base + j + 2, 8:72, :] = s
             hys[0, base + j] = s[0:2]
             hys[1, base + j] = s[62:64]
-            turned = roll(s, 64 * (c % 2) + 4 * j + 2, 1)
+            turned = roll(s, 32 * (c % 4) + 4 * j + 2, 1)
             packed = jnp.where(group == j, turned, packed)
         hzs[h] = packed
         return 0
 
     for c in range(chunks):
         sum_chunk(c, 0)
-        if c == 1:
+        if c == 3:
             near_done()
+            send(0, 0)
             for k in (2, 3):
-                send(k, 0)
-            send(0, 0)
-        if c > 0:
+                for early in range(3):
+                    send(k, early)
+        if c >= 3:
             for k in (2, 3):
                 send(k, c)
-        if c % 2:
+        if c % 4 == 3:
             for k in (4, 5):
                 send(k, c)
     send(1, 0)
-
     small[0].wait()
 
     def dz_chunk(c, _):
@@ -350,6 +358,63 @@
         return 0
 
     lax.fori_loop(0, 4, dz_chunk, 0, unroll=True)
+
+    groups = 16
+    slabs = groups + 3
+    even4 = 0.5 * (W4 + W4[::-1])
+    odd4 = 0.5 * (W4 - W4[::-1])
+
+    def column(axes):
+        per = 4
+
+        def one(yt, _):
+            r0 = pl.multiple_of(8 * yt, 8)
+
+            def put(a, g, value):
+                xs[pl.ds(r0, 8), pl.ds(pl.multiple_of((a * slabs + g) * 128, 128), 128)] = value
+
+            def some(gg, acc):
+                acc = [list(row) for row in acc]
+                x0 = 4 * per * gg
+                if 0 in axes:
+                    c = [sp[x0 + i, pl.ds(r0 + 8, 8), :] for i in range(4 * per + 4)]
+                for sub in range(per):
+                    force = [[] for _ in axes]
+                    for k in range(4):
+                        i = 4 * sub + k
+                        dv = diff[x0 + i, pl.ds(r0, 8), :]
+                        for n, a in enumerate(axes):
+                            if a == 0:
+                                s = (c[i] - c[i + 4]) + 8.0 * (c[i + 3] - c[i + 1])
+                            elif a == 1:
+                                ym2, ym1, yp1, yp2 = (
+                                    sp[x0 + i + 2, pl.ds(r0 + o, 8), :] for o in (6, 7, 9, 10))
+                                s = (ym2 - yp2) + 8.0 * (yp1 - ym1)
+                            else:
+                                s = dzb[x0 + i, pl.ds(r0, 8), :]
+                            force[n].append(dv * s)
+                    for n, a in enumerate(axes):
+                        f = force[n]
+                        e0, e1, o0, o1 = f[0] + f[3], f[1] + f[2], f[0] - f[3], f[1] - f[2]
+                        for m in range(2):
+                            both = float(even4[0, m]) * e0 + float(even4[1, m]) * e1
+                            diff4 = float(odd4[0, m]) * o0 + float(odd4[1, m]) * o1
+                            acc[n][m] = acc[n][m] + (both + diff4)
+                            acc[n][3 - m] = acc[n][3 - m] + (both - diff4)
+                        put(a, per * gg + sub, acc[n][0])
+                        acc[n] = [acc[n][1], acc[n][2], acc[n][3], zero8]
+                return tuple(tuple(row) for row in acc)
+
+            acc = lax.fori_loop(0, groups // per, some, tuple(tuple(zero8 for _ in range(4)) for _ in axes))
+            for n, a in enumerate(axes):
+                for m in range(3):
+                    put(a, groups + m, acc[n][m])
+            return 0
+
+        return one
+
+    lax.fori_loop(1, 7, column((0, 1)), 0)
+    lax.fori_loop(0, 2, lambda i, _: column((0,))(7 * i, 0), 0)
 
     for side, d in ((0, -1), (1, 1)):
         for axis, ref in enumerate((fxr, fyr, fzr)):
@@ -361,6 +426,122 @@
             @pl.when(jnp.logical_not(seen(-dx, -dy)))
             def _(dx=dx, dy=dy):
                 crecv[3 * (dx + 1) + dy + 1] = zero8
+
+    for k in range(6):
+        arrived(halo, k)
+
+    def place_y(x, _):
+        sp[x + 2, 6:8, :] = hyr[0, x]
+        sp[x + 2, 72:74, :] = hyr[1, x]
+        return 0
+
+    lax.fori_loop(0, 64, place_y, 0, unroll=8)
+
+    m4 = lane64 % 4
+    for h in range(2):
+        u = jnp.where(m4 < 2, hzr[0, h], hzr[1, h])
+        a_part = jnp.where(m4 < 2, -roll(u, -2, 1), roll(u, 2, 1))
+        b_part = jnp.where(m4 == 1, 8.0 * roll(u, -1, 1), jnp.where(m4 == 2, -8.0 * roll(u, 1, 1), 0.0))
+        cz[h] = a_part + b_part
+    plane = sorted(((ox, oy) for ox in range(nx) for oy in range(ny) if ox or oy),
+                   key=lambda o: -min(o[1], ny - o[1]) - 0.5 * min(o[0], nx - o[0]))
+
+    def in_plane(ox, oy):
+        return (lax.rem(gx + ox, nx), lax.rem(gy + oy, ny), gz)
+
+    def fine_copy(k):
+        axis, side = k // 2, k % 2
+        d = [0, 0, 0]
+        d[axis] = 2 * side - 1
+        if axis == 0:
+            src, dst = e.at[:, pl.ds(10 * side, 2)], fxr.at[1 - side]
+        elif axis == 1:
+            src, dst = fys.at[side], fyr.at[1 - side]
+        else:
+            src, dst = fzs.at[side], fzr.at[1 - side]
+        return d, pltpu.make_async_remote_copy(
+            src_ref=src, dst_ref=dst, send_sem=fs.at[k], recv_sem=fr.at[k],
+            device_id=at(d), device_id_type=MESH)
+
+    small[2].wait()
+
+    def z_fix(c, _):
+        base = pl.multiple_of(c * 16, 16)
+        layer = cz[c // 2]
+        for half in range(2):
+            group = lane64 // 4 - 16 * lax.rem(c, 2) - 8 * half
+            parts = [jnp.concatenate(split(jnp.where(group == j, layer, 0.0)), 1) for j in range(8)]
+            out = jnp.dot(jnp.concatenate(parts, 0), h_w[...], preferred_element_type=F32)
+            for j in range(8):
+                dzb[base + 8 * half + j] = dzb[base + 8 * half + j] + out[64 * j : 64 * (j + 1)]
+        return 0
+
+    lax.fori_loop(0, 4, z_fix, 0, unroll=True)
+
+    outer = (
+        (0, diff[0] * (hxr[0, 0] - 8.0 * hxr[0, 1]), diff[1] * hxr[0, 1], 0),
+        (groups - 1, diff[62] * -hxr[1, 0], diff[63] * (8.0 * hxr[1, 0] - hxr[1, 1]), 2),
+    )
+    for g, f0, f1, k in outer:
+        for m in range(4):
+            part = slice(128 * (g + m), 128 * (g + m + 1))
+            xs[:, part] = xs[:, part] + (float(W4[k, m]) * f0 + float(W4[k + 1, m]) * f1)
+
+    lax.fori_loop(1, 7, column((2,)), 0)
+    lax.fori_loop(0, 2, lambda i, _: column((1, 2))(7 * i, 0), 0)
+
+    for copy in small[3:]:
+        copy.wait()
+    total = None
+    for a in range(3):
+        x = xs[:, a * slabs * 128 : (a + 1) * slabs * 128]
+        hi, lo = split(x)
+        y = jnp.dot(wy[...], jnp.concatenate([hi, lo], 0), preferred_element_type=F32)
+        y = y[:24] + y[24:]
+        pieces = [y[:, 128 * i : 128 * (i + 1)] for i in range(slabs)]
+        hi, lo = split(jnp.concatenate([p[16:24] for p in pieces], 0))
+        z = jnp.dot(jnp.concatenate([hi, lo], 1), wz[1 + a], preferred_element_type=F32)
+        z = z[:, :128] + z[:, 128:]
+        total = z if total is None else total + z
+        for i in range(slabs):
+            zs[a, i] = pieces[i][:16]
+
+    lane8 = lanes((8, 128))
+    taken = []
+    for jj in range(6):
+        v = None
+        for i in range(slabs):
+            tap = i - 8 * jj + 25
+            if 0 <= tap < 29:
+                term = float(C29[tap]) * total[8 * i : 8 * (i + 1)]
+                v = term if v is None else v + term
+        taken.append(v)
+    for g in range(3):
+        v = jnp.where(lane8 < 64, taken[2 * g], taken[2 * g + 1])
+        csend[g] = jnp.where(lane8 // 32 % 2 == 0, v, roll(v, -1, 0))
+    crecv[4, pl.ds(gz, 1), :] = csend[1, 2:3, :]
+
+    def coarse_copy(dx, dy, o):
+        slot = 3 * (dx + 1) + dy + 1
+        return pltpu.make_async_remote_copy(
+            src_ref=csend.at[dx + 1, pl.ds(2 * (dy + 1), 1), :], dst_ref=crecv.at[slot, pl.ds(gz, 1), :],
+            send_sem=cs.at[slot], recv_sem=cr.at[slot], device_id=beside(dx, dy, o), device_id_type=MESH)
+
+    def coarse_line(dx, dy):
+        slot = 3 * (dx + 1) + dy + 1
+        rows = crecv.at[slot] if dx or dy else crecv.at[slot, pl.ds(0, nz - 1), :]
+        return pltpu.make_async_remote_copy(
+            src_ref=rows, dst_ref=rows, send_sem=cs.at[slot], recv_sem=cr.at[slot],
+            device_id=beside(0, 0, 1), device_id_type=MESH)
+
+    def coarse_all(fn):
+        for o in ring_order(nz):
+            for dx, dy in sorted(sides, key=lambda d: -abs(d[0]) - abs(d[1])):
+                if o or dx or dy:
+                    fn(dx, dy, o)
+
+    far_done()
+    coarse_all(lambda dx, dy, o: if_seen(dx, dy, lambda: coarse_copy(dx, dy, o).start()))
 
     small[1].wait()
 
@@ -406,162 +587,16 @@
 
     lax.fori_loop(0, 3, fine_bend, 0)
 
-    for k in range(6):
-        arrived(halo, k)
-
-    def place_y(x, _):
-        sp[x + 2, 6:8, :] = hyr[0, x]
-        sp[x + 2, 72:74, :] = hyr[1, x]
-        return 0
-
-    lax.fori_loop(0, 64, place_y, 0, unroll=8)
-
-    m4 = lane64 % 4
-    for h in range(2):
-        u = jnp.where(m4 < 2, hzr[0, h], hzr[1, h])
-        a_part = jnp.where(m4 < 2, -roll(u, -2, 1), roll(u, 2, 1))
-        b_part = jnp.where(m4 == 1, 8.0 * roll(u, -1, 1), jnp.where(m4 == 2, -8.0 * roll(u, 1, 1), 0.0))
-        cz[h] = a_part + b_part
-    plane = sorted(((ox, oy) for ox in range(nx) for oy in range(ny) if ox or oy),
-                   key=lambda o: -min(o[1], ny - o[1]) - 0.5 * min(o[0], nx - o[0]))
-
-    def in_plane(ox, oy):
-        return (lax.rem(gx + ox, nx), lax.rem(gy + oy, ny), gz)
-
-    def fine_copy(k):
-        axis, side = k // 2, k % 2
-        d = [0, 0, 0]
-        d[axis] = 2 * side - 1
-        if axis == 0:
-            src, dst = e.at[:, pl.ds(10 * side, 2)], fxr.at[1 - side]
-        elif axis == 1:
-            src, dst = fys.at[side], fyr.at[1 - side]
-        else:
-            src, dst = fzs.at[side], fzr.at[1 - side]
-        return d, pltpu.make_async_remote_copy(
-            src_ref=src, dst_ref=dst, send_sem=fs.at[k], recv_sem=fr.at[k],
-            device_id=at(d), device_id_type=MESH)
-
-    small[2].wait()
-
-    def z_fix(c, _):
-        base = pl.multiple_of(c * 16, 16)
-        layer = cz[c // 2]
-        for half in range(2):
-            group = lane64 // 4 - 16 * lax.rem(c, 2) - 8 * half
-            parts = [jnp.concatenate(split(jnp.where(group == j, layer, 0.0)), 1) for j in range(8)]
-            out = jnp.dot(jnp.concatenate(parts, 0), h_w[...], preferred_element_type=F32)
-            for j in range(8):
-                dzb[base + 8 * half + j] = dzb[base + 8 * half + j] + out[64 * j : 64 * (j + 1)]
-        return 0
-
-    lax.fori_loop(0, 4, z_fix, 0, unroll=True)
-
-    groups = 16
-    slabs = groups + 3
-
-    def column(yt, _):
-        r0 = pl.multiple_of(8 * yt, 8)
-
-        def put(a, g, value):
-            xs[pl.ds(r0, 8), pl.ds(pl.multiple_of((a * slabs + g) * 128, 128), 128)] = value
-
-        def pair(gg, acc):
-            acc = [list(row) for row in acc]
-            x0 = 8 * gg
-            c = [sp[x0 + i, pl.ds(r0 + 8, 8), :] for i in range(12)]
-            for sub in range(2):
-                for k in range(4):
-                    i = 4 * sub + k
-                    plane = x0 + i + 2
-                    sx = (c[i] - c[i + 4]) + 8.0 * (c[i + 3] - c[i + 1])
-                    ym2 = sp[plane, pl.ds(r0 + 6, 8), :]
-                    ym1 = sp[plane, pl.ds(r0 + 7, 8), :]
-                    yp1 = sp[plane, pl.ds(r0 + 9, 8), :]
-                    yp2 = sp[plane, pl.ds(r0 + 10, 8), :]
-                    sy = (ym2 - yp2) + 8.0 * (yp1 - ym1)
-                    sz = dzb[x0 + i, pl.ds(r0, 8), :]
-                    dv = diff[x0 + i, pl.ds(r0, 8), :]
-                    for a, s in enumerate((sx, sy, sz)):
-                        f = dv * s
-                        for m in range(4):
-                            acc[a][m] = acc[a][m] + float(W4[k, m]) * f
-                for a in range(3):
-                    put(a, 2 * gg + sub, acc[a][0])
-                    acc[a] = [acc[a][1], acc[a][2], acc[a][3], jnp.zeros((8, 128), F32)]
-            return tuple(tuple(row) for row in acc)
-
-        acc = lax.fori_loop(0, groups // 2, pair, tuple(tuple(zero8 for _ in range(4)) for _ in range(3)))
-        for a in range(3):
-            for m in range(3):
-                put(a, groups + m, acc[a][m])
-        return 0
-
-    lax.fori_loop(0, 8, column, 0)
-
-    for copy in small[3:]:
-        copy.wait()
-    total = None
     for a in range(3):
-        x = xs[:, a * slabs * 128 : (a + 1) * slabs * 128]
-        hi, lo = split(x)
-        y = jnp.dot(wy[...], jnp.concatenate([hi, lo], 0), preferred_element_type=F32)
-        y = y[:24] + y[24:]
-        pieces = [y[:, 128 * i : 128 * (i + 1)] for i in range(slabs)]
-        hi, lo = split(jnp.concatenate([p[16:24] for p in pieces], 0))
-        z = jnp.dot(jnp.concatenate([hi, lo], 1), wz[1 + a], preferred_element_type=F32)
-        z = z[:, :128] + z[:, 128:]
-        total = z if total is None else total + z
-        hi, lo = split(jnp.concatenate([p[:16] for p in pieces], 0))
+        hi, lo = split(zs[a].reshape(16 * slabs, 128))
         z = jnp.dot(jnp.concatenate([hi, lo], 1), wz[0], preferred_element_type=F32)
         z = z[:, :128] + z[:, 128:]
-        for i in range(slabs):
-            zs[a, i] = z[16 * i : 16 * (i + 1)]
-
-    lane8 = lanes((8, 128))
-    taken = []
-    for jj in range(6):
-        v = None
-        for i in range(slabs):
-            tap = i - 8 * jj + 25
-            if 0 <= tap < 29:
-                term = float(C29[tap]) * total[8 * i : 8 * (i + 1)]
-                v = term if v is None else v + term
-        taken.append(v)
-    for g in range(3):
-        v = jnp.where(lane8 < 64, taken[2 * g], taken[2 * g + 1])
-        csend[g] = jnp.where(lane8 // 32 % 2 == 0, v, roll(v, -1, 0))
-    crecv[4, pl.ds(gz, 1), :] = csend[1, 2:3, :]
-
-    def coarse_copy(dx, dy, o):
-        slot = 3 * (dx + 1) + dy + 1
-        return pltpu.make_async_remote_copy(
-            src_ref=csend.at[dx + 1, pl.ds(2 * (dy + 1), 1), :], dst_ref=crecv.at[slot, pl.ds(gz, 1), :],
-            send_sem=cs.at[slot], recv_sem=cr.at[slot], device_id=beside(dx, dy, o), device_id_type=MESH)
-
-    def coarse_line(dx, dy):
-        slot = 3 * (dx + 1) + dy + 1
-        rows = crecv.at[slot] if dx or dy else crecv.at[slot, pl.ds(0, nz - 1), :]
-        return pltpu.make_async_remote_copy(
-            src_ref=rows, dst_ref=rows, send_sem=cs.at[slot], recv_sem=cr.at[slot],
-            device_id=beside(0, 0, 1), device_id_type=MESH)
-
-    def coarse_all(fn):
-        for o in ring_order(nz):
-            for dx, dy in sorted(sides, key=lambda d: -abs(d[0]) - abs(d[1])):
-                if o or dx or dy:
-                    fn(dx, dy, o)
-
-    far_done()
-    coarse_all(lambda dx, dy, o: if_seen(dx, dy, lambda: coarse_copy(dx, dy, o).start()))
-
-    for a in range(3):
         for j in range(12):
             v = e[a, j]
             for k in range(5):
                 i = 2 * j - 4 + k
                 if 0 <= i < slabs:
-                    v = v + float(TWO[k]) * zs[a, i]
+                    v = v + float(TWO[k]) * z[16 * i : 16 * (i + 1)]
             e[a, j] = v
     for k in (0, 1):
         start(fine_copy, k)
@@ -706,11 +741,11 @@
             v(*fine_control.shape), v(*coarse_control.shape), h(2 * sz, sz), h(256, sz), h(48, 2 * sy),
             h(4, 2 * sz, 256), dma((6,)), v(sx, sy, sz), v(sx, sy, sz), v(sx + 4, sy + 16, sz), v(sx, sy, sz),
             v(sx, sy, sz), v(2, sy, 128), v(3, 12, 16, 128),
-            v(2, sx, 2, sz), v(2, sx, 2, sz), v(2, sy, 128), v(2, 2, sy, 128), v(12, 16, 128),
+            v(2, 2, sy, sz), v(2, sx, 2, sz), v(2, sx, 2, sz), v(2, sy, 128), v(2, 2, sy, 128), v(12, 16, 128),
             v(sy, 3 * slabs * 128), v(3, slabs, 16, 128), v(3, 8, 128), v(9, nz, 128),
             v(nx, 3, ny, 128), v(3 * (nx * ny - 1), 128), v(3, kx, ky, 128),
             v(2, 3, 2, 16, 128), v(2, 24, 2, 128), v(2, 24, 2, 128), v(2, 8, 128), v(2, 8, 128),
-            dma((2, 4)), dma((6,)), dma((6,)), dma((9,)), dma((9,)), dma, dma, dma((6,)), dma((6,)), flag, flag,
+            dma((2, 8)), dma((6,)), dma((6,)), dma((9,)), dma((9,)), dma, dma, dma((6,)), dma((6,)), flag, flag,
         ],
         compiler_params=pltpu.CompilerParams(collective_id=0, has_side_effects=True, vmem_limit_bytes=48 << 20),
         name="gradient",

time: 38.4 us -> 36.7 us (0.956)
  Pallas kernels: 36.3 us -> 34.5 us
    pallas_call x1, Pallas kernels: 36.3 us -> 34.5 us  [per_device(): pl.pallas_call(lambda *refs: gradient(dims, *refs), out_shape=(out(*fine_...]
where the time goes in v4:
time: 36.7 us; the launch traced here: 36.5 us
  Pallas kernels  34.5 us (94%)
  local copies, waits for them, and re-layouts  1.39 us (4%)
  between operations  0.64 us (2%)
    pallas_call x1, Pallas kernels, per_device(): pl.pallas_call(lambda *refs: gradient(dims, *refs), out_shape=(out(*fine_...  34.5 us
    unnamed x2, local copies, waits for them, and re-layouts  1.39 us

profile of v4, /device:TPU:1, one launch (start us, length us, event | category | flops | bytes accessed | tf_op | source)
XLA Modules:
  0.0 36.5 jit_solution(282663977194263675)
XLA Ops:
  0.6 34.5 %gradient.1 = (f32[3,8,8,16]{3,2,1,0:T(8,128)S(1)}, f32[3,16,16,32]{3,2,1,0:T(8,128)S(1)}) custom-call(f32[64,64,128]{2,1,0:T(8,128)} %refs_0_.1, f32[64,64,128]{2,1,0:T(8,128)} %refs_1_.1, f32[3,8,8,16]{3,2,1,0:T(8,128)} %refs_2_.1, f32[3,16,16,32]{3,2,1,0:T(8,128)} %refs_3_.1, bf16[256,128]{1,0:T(8,128)(2,1)} %constant.8.clone.refs_4_, ...), custom_call_target="tpu_custom_call" | custom-call | tf_op jit(solution)/shard_map/gradient/pallas_call | solution.py:735
  35.2 0.6 %copy.12 = f32[3,8,8,16]{3,2,1,0:T(8,128)} copy(f32[3,8,8,16]{3,2,1,0:T(8,128)S(1)} %get-tuple-element.4) | data formatting | bytes 24576
  35.8 0.7 %copy.13 = f32[3,16,16,32]{3,2,1,0:T(8,128)} copy(f32[3,16,16,32]{3,2,1,0:T(8,128)S(1)} %get-tuple-element.5) | data formatting | bytes 196608

commit v5 on v4

--- a/solution.py
+++ b/solution.py
@@ -719,6 +719,14 @@
     gather_plane().wait_send()
 
 
+def write_out(fine, coarse, fine_out, coarse_out, sem):
+    copies = [pltpu.make_async_copy(coarse, coarse_out, sem.at[0]), pltpu.make_async_copy(fine, fine_out, sem.at[1])]
+    for copy in copies:
+        copy.start()
+    for copy in copies:
+        copy.wait()
+
+
 def per_device(dims, warped_image, fixed_image, fine_control, coarse_control):
     sx, sy, sz = warped_image.shape
     kx, ky, kz = coarse_control.shape[1:]
@@ -732,7 +740,7 @@
     dma = pltpu.SemaphoreType.DMA
     flag = pltpu.SemaphoreType.REGULAR
     far = lambda x: pltpu.with_memory_space_constraint(jnp.asarray(x), pltpu.HBM)
-    return pl.pallas_call(
+    results = pl.pallas_call(
         lambda *refs: gradient(dims, *refs),
         out_shape=(out(*fine_control.shape), out(*coarse_control.shape)),
         in_specs=[hbm] * 8,
@@ -751,6 +759,15 @@
         name="gradient",
     )(far(warped_image), far(fixed_image), far(fine_control), far(coarse_control), far(d_matrix(sz)),
       far(h_matrix(sz)), far(y_matrix(sy)), far(z_matrices(sz)))
+    return pl.pallas_call(
+        write_out,
+        out_shape=(out(*fine_control.shape), out(*coarse_control.shape)),
+        in_specs=[vmem] * 2,
+        out_specs=(hbm, hbm),
+        scratch_shapes=[dma((2,))],
+        compiler_params=pltpu.CompilerParams(vmem_limit_bytes=1 << 20),
+        name="write_out",
+    )(*results)
 
 
 def solution(mesh):

time: 36.7 us -> 36.1 us (0.984)
  local copies, waits for them, and re-layouts: 1.39 us -> 0 us
  Pallas kernels: 34.5 us -> 35.3 us
    unnamed x2 -> x0, local copies, waits for them, and re-layouts: 1.39 us -> none
    pallas_call x0 -> x1, Pallas kernels: none -> 0.79 us  [per_device(): pl.pallas_call(write_out, out_shape=(out(*fine_control.shape), out(*coars...]
where the time goes in v5:
time: 36.1 us; the launch traced here: 35.9 us
  Pallas kernels  35.3 us (98%)
  between operations  0.64 us (2%)
    pallas_call x1, Pallas kernels, per_device(): pl.pallas_call(lambda *refs: gradient(dims, *refs), out_shape=(out(*fine_...  34.5 us
    pallas_call x1, Pallas kernels, per_device(): pl.pallas_call(write_out, out_shape=(out(*fine_control.shape), out(*coars...  0.79 us

profile of v5, /device:TPU:1, one launch (start us, length us, event | category | flops | bytes accessed | tf_op | source)
XLA Modules:
  0.0 35.9 jit_solution(11975160865284600706)
XLA Ops:
  0.6 34.5 %gradient.1 = (f32[3,8,8,16]{3,2,1,0:T(8,128)S(1)}, f32[3,16,16,32]{3,2,1,0:T(8,128)S(1)}) custom-call(f32[64,64,128]{2,1,0:T(8,128)} %refs_0_.1, f32[64,64,128]{2,1,0:T(8,128)} %refs_1_.1, f32[3,8,8,16]{3,2,1,0:T(8,128)} %refs_2_.1, f32[3,16,16,32]{3,2,1,0:T(8,128)} %refs_3_.1, bf16[256,128]{1,0:T(8,128)(2,1)} %constant.8.clone.refs_4_, ...), custom_call_target="tpu_custom_call" | custom-call | tf_op jit(solution)/shard_map/gradient/pallas_call | solution.py:743
  35.1 0.8 %write_out.1 = (f32[3,8,8,16]{3,2,1,0:T(8,128)}, f32[3,16,16,32]{3,2,1,0:T(8,128)}) custom-call(f32[3,8,8,16]{3,2,1,0:T(8,128)S(1)} %get-tuple-element.4.fine, f32[3,16,16,32]{3,2,1,0:T(8,128)S(1)} %get-tuple-element.5.coarse), custom_call_target="tpu_custom_call" | custom-call | tf_op jit(solution)/shard_map/write_out/pallas_call | solution.py:762

commit v6 on v5

--- a/solution.py
+++ b/solution.py
@@ -626,6 +626,31 @@
 
     lax.fori_loop(0, 3, coarse_bend, 0)
 
+    for dx, dy in sides:
+        if_seen(-dx, -dy, lambda: coarse_line(dx, dy).wait_recv())
+    line = crecv[0]
+    for i in range(1, 9):
+        line = line + crecv[i]
+    line = pltpu.roll(line, 0, 1, stride=4, stride_axis=0)
+    place = lane8 % 32 + 2 - 4 * lax.broadcasted_iota(jnp.int32, (8, 128), 0)
+    for a in range(3):
+        piece = jnp.where((place >= 0) & (place < 8), roll(line, -2 - 8 * a, 1), 0.0)
+        xg[gx, a, pl.ds(gy, 1), :] = jnp.sum(piece, axis=0, keepdims=True)
+
+    def gather_copy(ox, oy, sx, sy):
+        slot = xg.at[sx, :, pl.ds(sy, 1), :]
+        return pltpu.make_async_remote_copy(
+            src_ref=slot, dst_ref=slot, send_sem=gs, recv_sem=gr,
+            device_id=in_plane(ox, oy), device_id_type=MESH)
+
+    def gather_plane():
+        return pltpu.make_async_remote_copy(
+            src_ref=total_rows, dst_ref=total_rows, send_sem=gs, recv_sem=gr,
+            device_id=in_plane(0, 1), device_id_type=MESH)
+
+    for ox, oy in plane:
+        gather_copy(ox, oy, gx, gy).start()
+
     for k in (0, 1):
         sent(fine_copy, k)
         arrived(fine_copy, k)
@@ -641,31 +666,6 @@
             fys[1, 8 * a + j] = v[10:12]
     for k in (2, 3):
         start(fine_copy, k)
-
-    for dx, dy in sides:
-        if_seen(-dx, -dy, lambda: coarse_line(dx, dy).wait_recv())
-    line = crecv[0]
-    for i in range(1, 9):
-        line = line + crecv[i]
-    line = pltpu.roll(line, 0, 1, stride=4, stride_axis=0)
-    place = lane8 % 32 + 2 - 4 * lax.broadcasted_iota(jnp.int32, (8, 128), 0)
-    for a in range(3):
-        piece = jnp.where((place >= 0) & (place < 8), roll(line, -2 - 8 * a, 1), 0.0)
-        xg[gx, a, pl.ds(gy, 1), :] = jnp.sum(piece, axis=0, keepdims=True)
-
-    def gather_copy(ox, oy, sx, sy):
-        slot = xg.at[sx, :, pl.ds(sy, 1), :]
-        return pltpu.make_async_remote_copy(
-            src_ref=slot, dst_ref=slot, send_sem=gs, recv_sem=gr,
-            device_id=in_plane(ox, oy), device_id_type=MESH)
-
-    def gather_plane():
-        return pltpu.make_async_remote_copy(
-            src_ref=total_rows, dst_ref=total_rows, send_sem=gs, recv_sem=gr,
-            device_id=in_plane(0, 1), device_id_type=MESH)
-
-    for ox, oy in plane:
-        gather_copy(ox, oy, gx, gy).start()
 
     for k in (2, 3):
         arrived(fine_copy, k)

time: 36.1 us -> 36.1 us (level)
  no operation moved by 1% of the time
where the time goes in v6:
time: 36.1 us; the launch traced here: 35.9 us
  Pallas kernels  35.3 us (98%)
  between operations  0.64 us (2%)
    pallas_call x1, Pallas kernels, per_device(): pl.pallas_call(lambda *refs: gradient(dims, *refs), out_shape=(out(*fine_...  34.5 us
    pallas_call x1, Pallas kernels, per_device(): pl.pallas_call(write_out, out_shape=(out(*fine_control.shape), out(*coars...  0.79 us

profile of v6, /device:TPU:1, one launch (start us, length us, event | category | flops | bytes accessed | tf_op | source)
XLA Modules:
  0.0 35.9 jit_solution(2485515893968614988)
XLA Ops:
  0.6 34.5 %gradient.1 = (f32[3,8,8,16]{3,2,1,0:T(8,128)S(1)}, f32[3,16,16,32]{3,2,1,0:T(8,128)S(1)}) custom-call(f32[64,64,128]{2,1,0:T(8,128)} %refs_0_.1, f32[64,64,128]{2,1,0:T(8,128)} %refs_1_.1, f32[3,8,8,16]{3,2,1,0:T(8,128)} %refs_2_.1, f32[3,16,16,32]{3,2,1,0:T(8,128)} %refs_3_.1, bf16[256,128]{1,0:T(8,128)(2,1)} %constant.8.clone.refs_4_, ...), custom_call_target="tpu_custom_call" | custom-call | tf_op jit(solution)/shard_map/gradient/pallas_call | solution.py:743
  35.1 0.8 %write_out.1 = (f32[3,8,8,16]{3,2,1,0:T(8,128)}, f32[3,16,16,32]{3,2,1,0:T(8,128)}) custom-call(f32[3,8,8,16]{3,2,1,0:T(8,128)S(1)} %get-tuple-element.4.fine, f32[3,16,16,32]{3,2,1,0:T(8,128)S(1)} %get-tuple-element.5.coarse), custom_call_target="tpu_custom_call" | custom-call | tf_op jit(solution)/shard_map/write_out/pallas_call | solution.py:762
